TPU v7x, 512 devices: a whole 4x8x8 slice. The times are simulated.
512 devices in a mesh: clip: 8 (over y), tm: 16 (over z_lo, x), mp: 4 (over z_hi, core).
Axes of the slice: x: 4, y: 8, z: 8 (z_hi: 2, z_lo: 4; z = z_hi * 4 + z_lo), core: 2. Of those that a mesh axis runs over, the one named last changes fastest.
Arguments:
- token_ids: int32 [128, 256], P(('clip', 'tm')), parts along dimension 0, may hold values from 0 to 1023
- remask: int32 [128, 256], P(('clip', 'tm')), parts along dimension 0, may hold values from -1 to 255, as said below
- position_embed: bfloat16 [16, 256, 1024], P('tm'), may hold values from -0.625 to 0.625
- mask_embed: bfloat16 [1024], replicated, may hold values from -0.625 to 0.625
- table: bfloat16 [1024, 1024], P('mp')
- gain_in: float32 [1024], replicated, may hold values from 0.5 to 1.5
- gain_out: float32 [1024], replicated, may hold values from 0.5 to 1.5
- w_qkv: bfloat16 [3, 1024, 1024], P(None, None, 'mp')
- w_out: bfloat16 [1024, 1024], P('mp'), may hold values from -0.1875 to 0.1875
Outputs:
- log_probs: bfloat16 [128, 256, 1024], P(('clip', 'tm'), None, 'mp'), parts along dimension 0
- confidence: float32 [128, 256], P(('clip', 'tm')), parts along dimension 0
- clip_stats: float32 [16], P('clip'), parts along dimension 0
There are 8 independent parts, one for each index of `clip`. A program takes and returns all parts, laid end to end along the dimension named above; an argument that names none is the same for every part. Nothing has to cross between parts.
Inputs may be any that keep to these rules, and one draw needn't show every extreme that they name: `remask`: row f lists distinct masked positions of frame f in its first slots and -1 in the unused ones; every frame lists at least one position.
All inputs are finite; a program needn't handle non-finite values.
Results may differ from a plain program's by a relative error of at most 0.019.
The roundings to bfloat16 on the way count: a program that leaves them out, or rounds other values in their place, can miss the bound.
Values may be sent and summed in bfloat16 or wider, within the bound.
A program may use at most 64 MiB of HBM per device.

v0:
```python
import math

import jax
import jax.numpy as jnp
from jax import lax
from jax.sharding import Mesh
from jax.sharding import PartitionSpec as P

HEAD_DIM = 64
TM = ("tm_0", "tm_1")
CLIP_TM = ("clip", "tm_0", "tm_1")


def split_up(array, dim, size):
    before, after = (array.shape[:dim], array.shape[dim + 1 :])
    return jnp.moveaxis(array.reshape(*before, size, -1, *after), dim, 0)


def sum_at_owner(array, axis, dim):
    size = lax.axis_size(axis)
    blocks = lax.all_to_all(split_up(array, dim, size), axis, 0, 0, tiled=True)
    return jnp.sum(blocks.astype(jnp.float32), axis=0)


def sent_to_all(array, axis):
    size = lax.axis_size(axis)
    return lax.all_to_all(
        jnp.broadcast_to(array[None], (size, *array.shape)), axis, 0, 0, tiled=True
    )


def laid_out(blocks, dim):
    lengths = list(blocks.shape[1:])
    lengths[dim] *= blocks.shape[0]
    return jnp.moveaxis(blocks, 0, dim).reshape(lengths)


def gathered_copies(array, axis, dim):
    blocks = sent_to_all(array, axis)
    return laid_out(blocks, dim)


def gather_axes(array, axes, dim):
    for axis in reversed(axes):
        array = lax.all_gather(array, axis, axis=dim, tiled=True)
    return array


def sum_at_owner_2(array, axis, dim):
    size = lax.axis_size(axis)
    blocks = lax.all_to_all(split_up(array, dim, size), axis, 0, 0, tiled=True)
    return jnp.sum(blocks, axis=0)


def gathered_once(array, axis):
    leaves = jax.tree.leaves(array)
    sequence = sorted(range(len(leaves)), key=lambda k: -leaves[k].size)
    width = (1, *leaves[sequence[0]].shape)[-1]
    lines = [
        jnp.pad(leaves[k].reshape(-1), (0, -leaves[k].size % width)).reshape(-1, width)
        for k in sequence
    ]
    both, at, found = (sent_to_all(jnp.concatenate(lines), axis), 0, {})
    for k, line in zip(sequence, lines):
        slab = both[:, at : at + len(line)].reshape(len(both), -1)
        found[k] = slab[:, : leaves[k].size].reshape(-1, *leaves[k].shape)
        at += len(line)
    numbers = iter(range(len(leaves)))
    return jax.tree.map(lambda _: found[next(numbers)], array)


def joined_by_halves(pieces, combine):
    while len(jax.tree.leaves(pieces)[0]) > 1:
        pieces = jax.vmap(combine)(
            *(jax.tree.map(lambda part: part[side::2], pieces) for side in (0, 1))
        )
    return jax.tree.map(lambda part: part[0], pieces)


def merged(array, axis, combine):
    pieces = gathered_once(array, axis)
    return joined_by_halves(pieces, combine)


def over_copies(array, axis):
    everything = sent_to_all(array, axis)
    return jnp.sum(everything, axis=0)


def in_one(arrays, axis):
    flat, at, finished = (jnp.concatenate([a.reshape(-1) for a in arrays]), 0, [])
    total = over_copies(flat, axis)
    for a in arrays:
        finished.append(total[at : at + a.size].reshape(a.shape))
        at += a.size
    return tuple(finished)


def layer_norm(values, gain):
    center = values - jnp.mean(values, axis=-1, keepdims=True)
    spread = jnp.mean(center * center, axis=-1, keepdims=True)
    return center * lax.rsqrt(spread + 1e-05) * gain


def absorb_block(state, query, key_block, value_block):
    running, totals, summed = state
    scores = jnp.einsum(
        "qhd,khd->hqk", query, key_block, preferred_element_type=jnp.float32
    ) * HEAD_DIM ** (-0.5)
    raised = jnp.maximum(running, jnp.max(scores, axis=-1))
    fade = jnp.exp(running - raised)
    weights = jnp.exp(scores - raised[:, :, None])
    totals = totals * fade + jnp.sum(weights, axis=-1)
    summed = summed * fade[:, :, None] + jnp.einsum(
        "hqk,khd->hqd",
        weights.astype(jnp.bfloat16),
        value_block,
        preferred_element_type=jnp.float32,
    )
    return (raised, totals, summed)


def sweep_keys(state, query, key_rows, value_rows):
    count = key_rows.shape[0]
    block = math.gcd(count, 512)
    heads_here = query.shape[1]
    key_blocks = key_rows.reshape(count // block, block, heads_here, HEAD_DIM)
    value_blocks = value_rows.reshape(count // block, block, heads_here, HEAD_DIM)

    def advance(inner, pair):
        return (absorb_block(inner, query, pair[0], pair[1]), None)

    state, ignored = lax.scan(advance, state, (key_blocks, value_blocks))
    return state


def empty_state(heads_here, row_count):
    return (
        jnp.full((heads_here, row_count), -1e30, jnp.float32),
        jnp.zeros((heads_here, row_count), jnp.float32),
        jnp.zeros((heads_here, row_count, HEAD_DIM), jnp.float32),
    )


def join_pairs(left, right):
    highest = jnp.maximum(left[0], right[0])
    return (highest, left[1] * jnp.exp(left[0] - highest) + right[1] * jnp.exp(right[0] - highest))


def body(token_ids, remask, position_embed, mask_embed, table, gain_in, gain_out, w_qkv, w_out):
    frames_here, frame_span = token_ids.shape
    row_count = frames_here * frame_span
    parts_mp = lax.axis_size("mp")
    vocab_here = table.shape[0]
    local_width = w_qkv.shape[2]
    heads_here = local_width // HEAD_DIM
    offset = lax.axis_index("mp") * vocab_here
    spots = jnp.arange(frame_span, dtype=jnp.int32)
    masked = jnp.any(remask[:, None, :] == spots[None, :, None], axis=-1).reshape(row_count)
    flat_ids = token_ids.reshape(row_count)
    entries = offset + jnp.arange(vocab_here, dtype=jnp.int32)
    onehot = ((flat_ids[:, None] == entries[None, :]) & jnp.logical_not(masked)[:, None]).astype(
        jnp.bfloat16
    )
    added_rows = jnp.where(masked[:, None], mask_embed.astype(jnp.float32)[None, :], 0.0)
    added_rows = added_rows + position_embed.reshape(row_count, -1).astype(jnp.float32)
    share = row_count // parts_mp
    first_row = lax.axis_index("mp") * share
    looked = sum_at_owner(
        jnp.dot(onehot, table, preferred_element_type=jnp.float32).astype(jnp.bfloat16), "mp", 0
    )
    hidden_in = looked + lax.dynamic_slice_in_dim(added_rows, first_row, share, 0)
    normed = layer_norm(hidden_in, gain_in).astype(jnp.bfloat16)
    projected = jnp.einsum(
        "rd,jdc->jrc", gathered_copies(normed, "mp", 0), w_qkv, preferred_element_type=jnp.float32
    ).astype(jnp.bfloat16)
    query = projected[0].reshape(row_count, heads_here, HEAD_DIM)
    keys = projected[1]
    values = projected[2]
    highest, totals, summed = sweep_keys(
        empty_state(heads_here, row_count),
        query,
        gather_axes(keys, ("tm_1", "tm_0"), 0),
        gather_axes(values, ("tm_1", "tm_0"), 0),
    )
    context = (
        (summed / totals[:, :, None])
        .transpose(1, 0, 2)
        .reshape(row_count, local_width)
        .astype(jnp.bfloat16)
    )
    mixed_rows = sum_at_owner_2(
        jnp.dot(context, w_out, preferred_element_type=jnp.float32), "mp", 0
    )
    final_local = layer_norm(hidden_in + mixed_rows, gain_out).astype(jnp.bfloat16)
    logits = lax.dot_general(
        gathered_copies(final_local, "mp", 0),
        table,
        (((1,), (1,)), ((), ())),
        preferred_element_type=jnp.float32,
    )
    local_max = jnp.max(logits, axis=-1)
    local_total = jnp.sum(jnp.exp(logits - local_max[:, None]), axis=-1)
    row_max, row_total = merged((local_max, local_total), "mp", join_pairs)
    log_total = row_max + jnp.log(row_total)
    log_probs = (
        (logits - log_total[:, None])
        .astype(jnp.bfloat16)
        .reshape(frames_here, frame_span, vocab_here)
    )
    confidence = jnp.exp(row_max - log_total)
    weight = masked.astype(jnp.float32)
    conf_sum, count = in_one((jnp.sum(confidence * weight), jnp.sum(weight)), TM)
    tokens_all = row_count * lax.axis_size(TM)
    clip_stats = jnp.stack([conf_sum / count, jnp.log(count / tokens_all)])
    return (log_probs, confidence.reshape(frames_here, frame_span), clip_stats)


def solution(mesh):
    finer = Mesh(
        mesh.devices.reshape(mesh.shape["clip"], 4, 4, mesh.shape["mp"]),
        ("clip", "tm_0", "tm_1", "mp"),
    )
    in_specs = (
        P(CLIP_TM, None),
        P(CLIP_TM, None),
        P(TM, None, None),
        P(),
        P("mp", None),
        P(),
        P(),
        P(None, None, "mp"),
        P("mp", None),
    )
    out_specs = (P(CLIP_TM, None, "mp"), P(CLIP_TM, None), P("clip"))
    return jax.shard_map(body, mesh=finer, in_specs=in_specs, out_specs=out_specs, check_vma=False)
```

profile of v0, /device:TPU:1, one launch (start us, length us, event | category | flops | bytes accessed | tf_op | source)
XLA Modules:
  0.0 300.6 jit_solution(9512362363498867711)
XLA Ops:
  7.2 0.9 fusion.20
  8.2 2.2 convolution_convert_fusion
  10.4 11.8 %all-to-all-start = ((bf16[4,64,1024]{2,1,0:T(8,128)(2,1)}), bf16[4,64,1024]{2,1,0:T(8,128)(2,1)S(1)}, u32[]{:S(2)}, u32[]{:S(2)}) async-start(bf16[4,64,1024]{2,1,0:T(8,128)(2,1)} %bitcast.2), calls=%async_computation | async-start | bytes 1048576 | tf_op jit(solution)/shard_map/all_to_all | solution.py:21
  22.2 11.9 %all-to-all-done = bf16[4,64,1024]{2,1,0:T(8,128)(2,1)S(1)} async-done(((bf16[4,64,1024]{2,1,0:T(8,128)(2,1)}), bf16[4,64,1024]{2,1,0:T(8,128)(2,1)S(1)}, u32[]{:S(2)}, u32[]{:S(2)}) %all-to-all-start) | async-done | bytes 524320 | tf_op jit(solution)/shard_map/all_to_all | solution.py:21
  34.2 0.2 fusion.32
  34.4 0.2 multiply_reduce_fusion.1
  34.7 0.1 multiply_convert_fusion.1
  34.9 20.7 %all_to_all.31 = bf16[4,64,1024]{2,1,0:T(8,128)(2,1)S(1)} all-to-all(bf16[4,64,1024]{2,1,0:T(8,128)(2,1)S(1)} %broadcast_in_dim.42), channel_id=1, replica_groups=mesh['clip'=8,'tm_0'=4,'tm_1'=4,'mp'=4] {'mp'}, dimensions={0} | all-to-all | bytes 1048576 | tf_op jit(solution)/shard_map/all_to_all | solution.py:27
  55.6 0.7 fusion.15
  56.4 18.7 %all-gather = bf16[1,1024,256]{1,2,0:T(8,128)(2,1)} all-gather(bf16[1,256,256]{1,2,0:T(8,128)(2,1)S(1)} %get-tuple-element.147), channel_id=2, replica_groups=mesh['clip'=8,'tm_0'=4,'tm_1'=4,'mp'=4] {'tm_0'}, dimensions={1}, use_global_device_ids=true | all-gather | bytes 655360 | tf_op jit(solution)/shard_map/all_gather | solution.py:45
  75.1 14.1 %all-gather.2 = bf16[1,1024,256]{1,2,0:T(8,128)(2,1)} all-gather(bf16[1,256,256]{1,2,0:T(8,128)(2,1)S(1)} %get-tuple-element.145), channel_id=4, replica_groups=mesh['clip'=8,'tm_0'=4,'tm_1'=4,'mp'=4] {'tm_0'}, dimensions={1}, use_global_device_ids=true | all-gather | bytes 655360 | tf_op jit(solution)/shard_map/all_gather | solution.py:45
  89.2 22.2 %all-gather.7.cloned.1.call-done = bf16[1,4096,256]{1,2,0:T(8,128)(2,1)} async-done(((bf16[1,1024,256]{1,2,0:T(8,128)(2,1)}), bf16[1,4096,256]{1,2,0:T(8,128)(2,1)}) %all-gather.7.cloned.1.call-update) | async-done | bytes 2097168 | tf_op jit(solution)/shard_map/all_gather | solution.py:45
  111.4 2.5 copy.54
  113.9 2.0 copy.40
  115.9 33.8 %all-gather.9.cloned.1.call-done = bf16[1,4096,256]{1,2,0:T(8,128)(2,1)} async-done(((bf16[1,1024,256]{1,2,0:T(8,128)(2,1)}), bf16[1,4096,256]{1,2,0:T(8,128)(2,1)}) %all-gather.9.cloned.1.call-update) | async-done | bytes 2097168 | tf_op jit(solution)/shard_map/all_gather | solution.py:45
  149.7 2.5 copy.55
  152.2 2.0 copy.41
  154.1 51.9 %while.15 = (s32[]{:T(128)}, f32[4,256]{1,0:T(4,128)S(1)}, f32[4,256]{1,0:T(4,128)S(1)}, f32[4,256,64]{1,2,0:T(8,128)S(1)}, bf16[8,512,4,64]{1,3,2,0:T(8,128)(2,...) while((s32[]{:T(128)}, f32[4,256]{1,0:T(4,128)S(1)}, ...), condition=%wide.region_7.8_spmd.clone, body=%wide.region_4.7_spmd.clone.sunk | while | flops 138613760 | bytes 15926405 | solution.py:133
  154.1 2.8 bitcast_reduce_fusion.2
  157.0 2.1 fusion.54
  159.1 0.1 copy-done.1
  159.2 1.5 convolution_add_fusion.2
  160.7 2.8 bitcast_reduce_fusion.2
  163.5 2.1 fusion.54
  165.7 1.5 convolution_add_fusion.2
  167.2 2.8 bitcast_reduce_fusion.2
  169.9 2.1 fusion.54
  172.1 0.1 copy-done.1
  172.2 1.5 convolution_add_fusion.2
  173.7 2.8 bitcast_reduce_fusion.2
  176.4 2.1 fusion.54
  178.6 0.1 copy-done.1
  178.6 1.5 convolution_add_fusion.2
  180.1 2.8 bitcast_reduce_fusion.2
  182.9 2.1 fusion.54
  185.1 1.5 convolution_add_fusion.2
  186.6 2.8 bitcast_reduce_fusion.2
  189.4 2.1 fusion.54
  191.6 1.5 convolution_add_fusion.2
  193.1 2.8 bitcast_reduce_fusion.2
  195.9 2.1 fusion.54
  198.1 1.5 convolution_add_fusion.2
  199.6 2.8 bitcast_reduce_fusion.2
  202.4 2.1 fusion.54
  204.6 1.5 convolution_add_fusion.2
  206.1 0.2 reshape.183
  206.3 0.3 fusion.16
  206.6 30.5 %all_to_all.32 = f32[4,64,1024]{2,1,0:T(8,128)S(1)} all-to-all(f32[4,64,1024]{2,1,0:T(8,128)S(1)} %fusion.16), channel_id=1, replica_groups=mesh['clip'=8,'tm_0'=4,'tm_1'=4,'mp'=4] {'mp'}, dimensions={0} | all-to-all | bytes 2097152 | tf_op jit(solution)/shard_map/all_to_all | solution.py:51
  237.1 0.8 reduce_sum.102
  237.9 1.2 fusion.34
  239.1 0.2 multiply_reduce_fusion
  239.4 0.1 multiply_convert_fusion
  239.5 20.0 %all_to_all.33 = bf16[4,64,1024]{2,1,0:T(8,128)(2,1)S(1)} all-to-all(bf16[4,64,1024]{2,1,0:T(8,128)(2,1)S(1)} %broadcast_in_dim.43), channel_id=1, replica_groups=mesh['clip'=8,'tm_0'=4,'tm_1'=4,'mp'=4] {'mp'}, dimensions={0} | all-to-all | bytes 1048576 | tf_op jit(solution)/shard_map/all_to_all | solution.py:27
  259.5 0.4 fusion.39
  260.0 10.4 %all_to_all.34 = f32[4,2,256]{2,1,0:T(2,128)S(1)} all-to-all(f32[4,2,256]{2,1,0:T(2,128)S(1)} %broadcast_in_dim.44), channel_id=1, replica_groups=mesh['clip'=8,'tm_0'=4,'tm_1'=4,'mp'=4] {'mp'}, dimensions={0} | all-to-all | bytes 16384 | tf_op jit(solution)/shard_map/all_to_all | solution.py:27
  270.6 0.6 fusion.28
  271.2 0.6 select_reduce_fusion
  271.8 1.4 pad_maximum_fusion.1
  273.1 0.6 broadcast_in_dim.45
  273.7 9.8 %all-to-all-start.5 = ((f32[16,1,2]{2,1,0:T(1,128)}), f32[16,1,2]{2,1,0:T(1,128)S(1)}, u32[]{:S(2)}, u32[]{:S(2)}) async-start(f32[16,1,2]{2,1,0:T(1,128)} %broadcast_in_dim.45), calls=%async_computation.5 | async-start | bytes 16384 | tf_op jit(solution)/shard_map/all_to_all | solution.py:27
  283.6 0.8 copy.45
  284.3 6.0 %all-to-all-done.5 = f32[16,1,2]{2,1,0:T(1,128)S(1)} async-done(((f32[16,1,2]{2,1,0:T(1,128)}), f32[16,1,2]{2,1,0:T(1,128)S(1)}, u32[]{:S(2)}, u32[]{:S(2)}) %all-to-all-start.5) | async-done | bytes 160 | tf_op jit(solution)/shard_map/all_to_all | solution.py:27
  290.4 0.7 fusion.38
  293.1 0.6 pad_maximum_fusion.2
  (83 shorter events, 1.4 us)
Async XLA Ops:
  7.2 48.4 %copy-start = (bf16[3,1024,256]{2,1,0:T(8,128)(2,1)S(1)}, bf16[3,1024,256]{2,1,0:T(8,128)(2,1)}, u32[]{:S(2)}) copy-start(bf16[3,1024,256]{2,1,0:T(8,128)(2,1)} %param.18) | copy-start | bytes 4718596
  7.2 15.0 %copy-start.7 = (bf16[1024]{0:T(1024)(128)(2,1)S(1)}, bf16[1024]{0:T(1024)(128)(2,1)}, u32[]{:S(2)}) copy-start(bf16[1024]{0:T(1024)(128)(2,1)} %param.14) | copy-start | bytes 6148
  7.2 27.0 %copy-start.4 = (bf16[1,256,1024]{2,1,0:T(8,128)(2,1)S(1)}, bf16[1,256,1024]{2,1,0:T(8,128)(2,1)}, u32[]{:S(2)}) copy-start(bf16[1,256,1024]{2,1,0:T(8,128)(2,1)} %param.13) | copy-start | bytes 1572868
  7.2 27.4 %copy-start.5 = (f32[1024]{0:T(1024)S(1)}, f32[1024]{0:T(1024)}, u32[]{:S(2)}) copy-start(f32[1024]{0:T(1024)} %param.16) | copy-start | bytes 12292
  10.4 23.7 %all-to-all-start = ((bf16[4,64,1024]{2,1,0:T(8,128)(2,1)}), bf16[4,64,1024]{2,1,0:T(8,128)(2,1)S(1)}, u32[]{:S(2)}, u32[]{:S(2)}) async-start(bf16[4,64,1024]{2,1,0:T(8,128)(2,1)} %bitcast.2), calls=%async_computation | async-start | bytes 1048576 | tf_op jit(solution)/shard_map/all_to_all | solution.py:21
  22.1 89.2 %all-gather.7.cloned.1.call-start = ((), (), s32[]{:S(2)}) async-start(), calls=%async_computation.6 | async-start | bytes 2621440 | tf_op jit(solution)/shard_map/all_gather | solution.py:45
  75.1 74.6 %all-gather.9.cloned.1.call-start = ((), (), s32[]{:S(2)}) async-start(), calls=%async_computation.7 | async-start | bytes 2621440 | tf_op jit(solution)/shard_map/all_gather | solution.py:45
  154.1 52.1 %copy-start.3 = (bf16[256,1024]{1,0:T(8,128)(2,1)S(1)}, bf16[256,1024]{1,0:T(8,128)(2,1)}, u32[]{:S(2)}) copy-start(bf16[256,1024]{1,0:T(8,128)(2,1)} %param.19) | copy-start | bytes 1572868
  157.0 2.2 copy-start.1
  163.5 2.2 copy-start.1
  169.9 2.2 copy-start.1
  176.4 2.2 copy-start.1
  182.9 2.2 copy-start.1
  189.4 2.2 copy-start.1
  195.9 2.2 copy-start.1
  202.4 2.2 copy-start.1
  206.6 32.7 %copy-start.6 = (f32[1024]{0:T(1024)S(1)}, f32[1024]{0:T(1024)}, u32[]{:S(2)}) copy-start(f32[1024]{0:T(1024)} %param.17) | copy-start | bytes 12292
  237.1 22.4 %copy-start.2 = (bf16[256,1024]{1,0:T(8,128)(2,1)S(1)}, bf16[256,1024]{1,0:T(8,128)(2,1)}, u32[]{:S(2)}) copy-start(bf16[256,1024]{1,0:T(8,128)(2,1)} %param.15) | copy-start | bytes 1572868
  273.7 16.6 %all-to-all-start.5 = ((f32[16,1,2]{2,1,0:T(1,128)}), f32[16,1,2]{2,1,0:T(1,128)S(1)}, u32[]{:S(2)}, u32[]{:S(2)}) async-start(f32[16,1,2]{2,1,0:T(1,128)} %broadcast_in_dim.45), calls=%async_computation.5 | async-start | bytes 16384 | tf_op jit(solution)/shard_map/all_to_all | solution.py:27
Sparse Core Ops, SparseCore 0:
  75.2 36.1 all-gather.6
  113.5 36.1 all-gather.8
where the time goes:
time: 302 us; the launch traced here: 301 us
  blocking collectives  114 us (38%)
  waiting for transfers between devices  73.8 us (24%)
  matrix products  37.5 us (12%)
  other arithmetic  24.3 us (8%)
  starting transfers between devices  21.6 us (7%)
  between operations  16.4 us (5%)
  local copies, waits for them, and re-layouts  12.3 us (4%)
    all_gather x2, waiting for transfers between devices, gather_axes(): array = lax.all_gather(array, axis, axis=dim, tiled=True)  55.9 us
    all_to_all x3, blocking collectives, sent_to_all(): lax.all_to_all(jnp.broadcast_to(array[None], (size, *array.shape)), axis,...  51.1 us
    all_gather x2, blocking collectives, gather_axes(): array = lax.all_gather(array, axis, axis=dim, tiled=True)  32.7 us
    all_to_all x1, blocking collectives, sum_at_owner_2(): blocks = lax.all_to_all(split_up(array, dim, size), axis, 0, 0, tiled=True)  30.5 us
    dot_general x8, matrix products, absorb_block(): jnp.einsum('qhd,khd->hqk', query, key_block, preferred_element_type=jnp.f...  22.2 us
    reduce_sum x8, other arithmetic, absorb_block(): totals = totals * fade + jnp.sum(weights, axis=-1)  16.8 us
    all_to_all x1, waiting for transfers between devices, sum_at_owner(): blocks = lax.all_to_all(split_up(array, dim, size), axis, 0, 0, tiled=True)  11.9 us
    all_to_all x1, starting transfers between devices, sum_at_owner(): blocks = lax.all_to_all(split_up(array, dim, size), axis, 0, 0, tiled=True)  11.8 us
  transfers between devices with their start and end apart: 4, of which 4 were waited for; matrix products, arithmetic and copies ran while one was open for 2% of the time, Pallas kernels for 0%

commit v1 on v0

v1 whole, which is shorter than its diff:
```python
import math

import jax
import jax.numpy as jnp
from jax import lax
from jax.experimental import pallas as pl
from jax.experimental.pallas import tpu as pltpu
from jax.sharding import Mesh
from jax.sharding import PartitionSpec as P

HEAD_DIM = 64
MESH = pl.DeviceIdType.MESH
AXES = ("clip", "zl", "x", "zh", "core")
BF = jnp.bfloat16
F32 = jnp.float32
SCALE = HEAD_DIM**-0.5 * math.log2(math.e)


def coords():
    return [lax.axis_index(name) for name in AXES]


def at(y, zl, x, zh, core):
    mine = coords()
    sizes = (8, 4, 4, 2, 2)
    return tuple(
        lax.rem(mine[k] + step + sizes[k], sizes[k]) if step else mine[k]
        for k, step in enumerate((y, zl, x, zh, core))
    )


def mirror():
    y, zl, x, zh, core = coords()
    return (y, 3 - zl, x, 1 - zh, core)


def remote(src, dst, send, recv, device):
    return pltpu.make_async_remote_copy(
        src_ref=src, dst_ref=dst, send_sem=send, recv_sem=recv, device_id=device, device_id_type=MESH
    )


def arrived(ref, sem):
    remote(ref, ref, sem, sem, at(0, 0, 0, 0, 1)).wait_recv()


def left(ref, sem):
    remote(ref, ref, sem, sem, at(0, 0, 0, 0, 1)).wait_send()


def norm_rows(h, gain):
    center = h - jnp.mean(h, axis=-1, keepdims=True)
    spread = jnp.mean(center * center, axis=-1, keepdims=True)
    return center * lax.rsqrt(spread + 1e-05) * gain


class Spread:
    def __init__(self, hbm, full, ssem, zsem, ysem, xsem, dsem):
        self.hbm, self.full = hbm, full
        self.ssem, self.zsem, self.ysem, self.xsem, self.dsem = ssem, zsem, ysem, xsem, dsem
        y, zl, x, zh, core = coords()
        self.y, self.x = y, x
        self.own = zh * 2 + core
        self.got = (1 - zh) * 2 + core

    def rows(self, quarter, x):
        return pl.ds(pl.multiple_of(quarter * 256 + x * 64, 64), 64)

    def cols(self, y):
        return pl.ds(pl.multiple_of(y * 128, 128), 128)

    def local(self):
        quarter = pl.ds(pl.multiple_of(self.own * 256, 256), 256)
        return pltpu.make_async_copy(self.hbm, self.full.at[quarter], self.ssem.at[4])

    def start_z(self):
        src = self.hbm.at[pl.ds(pl.multiple_of(self.x * 64, 64), 64), self.cols(self.y)]
        dst = self.full.at[self.rows(self.own, self.x), self.cols(self.y)]
        remote(src, dst, self.ssem.at[0], self.zsem, mirror()).start()

    def start_own_quarter(self):
        quarter = pl.ds(pl.multiple_of(self.own * 256, 256), 256)
        remote(
            self.hbm, self.full.at[quarter], self.ssem.at[3], self.dsem.at[0], at(0, 0, 0, 0, 1)
        ).start()

    def forward_x(self, y):
        piece = self.full.at[self.rows(self.got, self.x), self.cols(y)]
        for dx in (1, 3, 2):
            remote(piece, piece, self.ssem.at[2], self.xsem.at[dx], at(0, 0, dx, 0, 0)).start()

    def start_y(self):
        piece = self.full.at[self.rows(self.got, self.x), self.cols(self.y)]
        arrived(piece, self.zsem)
        for dy in (4, 3, 5, 2, 6, 1, 7):
            remote(piece, piece, self.ssem.at[1], self.ysem.at[dy], at(dy, 0, 0, 0, 0)).start()
        self.forward_x(self.y)

    def start_x(self):
        for dy in (1, 7, 2, 6, 3, 5, 4):
            source = lax.rem(self.y - dy + 8, 8)
            piece = self.full.at[self.rows(self.got, self.x), self.cols(source)]
            arrived(piece, self.ysem.at[dy])
            self.forward_x(source)
        self.hand_over(self.x)

    def hand_over(self, x):
        block = self.full.at[self.rows(self.got, x)]
        remote(block, block, self.ssem.at[3], self.dsem.at[1], at(0, 0, 0, 0, 1)).start()

    def finish_x(self):
        for dx in (1, 3, 2):
            x = lax.rem(self.x - dx + 4, 4)
            arrived(self.full.at[self.rows(self.got, x)], self.xsem.at[dx])
            self.hand_over(x)

    def wait_all(self):
        quarter = self.full.at[pl.ds(0, 256)]
        arrived(quarter, self.dsem.at[0])
        arrived(quarter, self.dsem.at[1])

    def wait_sent(self):
        left(self.full.at[pl.ds(0, 64), pl.ds(0, 128)], self.ssem.at[0])
        left(self.full.at[pl.ds(0, 64), pl.ds(0, 896)], self.ssem.at[1])
        left(self.full.at[pl.ds(0, 192)], self.ssem.at[2])
        left(self.full.at[pl.ds(0, 512)], self.ssem.at[3])


def kernel(
    ids_ref, remask_ref, mask_embed_ref, gain_in_ref, gain_out_ref, table_hbm, wqkv_hbm, wout_hbm, pos_hbm,
    logp_ref, conf_ref, stats_ref,
    table, wout, wqkv, pos, hidden, normed, kv_out, q_out, kv, q_in, qpad, high, total, summed, o_out, ctx,
    final, logits, weight, stat_out, stat_in,
    local_sem, t_s, t_z, t_y, t_x, t_d, w_s, w_z, w_y, w_x, w_d, a_send, a_recv, q_recv, b_send, b_recv,
    c_send, c_recv, f_send, f_recv, s_send, s_recv,
):
    y, zl, x, zh, core = coords()
    mp = zh * 2 + core
    frame = zl * 4 + x
    tab = Spread(table_hbm, table, t_s, t_z, t_y, t_x, t_d)
    out = Spread(wout_hbm, wout, w_s, w_z, w_y, w_x, w_d)
    load_pos = pltpu.make_async_copy(pos_hbm.at[0], pos, local_sem.at[0])
    load_qkv = pltpu.make_async_copy(wqkv_hbm, wqkv, local_sem.at[1])

    barrier = pltpu.get_barrier_semaphore()
    peers = []
    for k in range(1, 16):
        place = lax.rem(zh * 8 + zl * 2 + core + k, 16)
        peers.append((y, lax.rem(place // 2, 4), x, place // 8, lax.rem(place, 2)))
    peers += [at(k, 0, 0, 0, 0) for k in range(1, 8)]
    peers += [at(0, dz, dx, 0, 0) for dx in range(1, 4) for dz in range(4)]
    for peer in peers:
        pl.semaphore_signal(barrier, inc=1, device_id=peer, device_id_type=MESH)
    tab.local().start()
    load_pos.start()
    load_qkv.start()
    out.local().start()

    row = lax.broadcasted_iota(jnp.int32, (256, 256), 0)
    lane = lax.broadcasted_iota(jnp.int32, (256, 256), 1)
    masked = jnp.max(jnp.where(remask_ref[...] == row, 1.0, 0.0), axis=1, keepdims=True)
    ids_col = jnp.sum(
        jnp.where(row == lane, ids_ref[...].astype(F32), 0.0), axis=1, keepdims=True
    )
    weight[...] = jnp.broadcast_to(masked, (256, 128))
    entry = lax.broadcasted_iota(jnp.int32, (256, 1024), 1).astype(F32)
    onehot = jnp.where(entry == jnp.where(masked > 0.5, -1.0, ids_col), 1.0, 0.0).astype(BF)

    pl.semaphore_wait(barrier, len(peers))
    tab.start_z()
    out.start_z()
    tab.start_own_quarter()
    tab.start_y()
    out.start_y()
    tab.start_x()
    tab.finish_x()
    out.start_own_quarter()
    out.start_x()
    tab.local().wait()
    load_pos.wait()
    load_qkv.wait()
    tab.wait_all()

    hidden[...] = jnp.dot(onehot, table[...], preferred_element_type=F32)
    mask_row = mask_embed_ref[...].astype(F32)
    gain_in = gain_in_ref[...]

    def first_norm(k, carry):
        block = pl.ds(pl.multiple_of(k * 64, 64), 64)
        h = hidden[block] + jnp.where(weight[block][:, :1] > 0.5, mask_row, 0.0)
        h = h + pos[block].astype(F32)
        hidden[block] = h
        normed[block] = norm_rows(h, gain_in).astype(BF)
        return carry

    lax.fori_loop(0, 4, first_norm, 0)
    low = lax.broadcasted_iota(jnp.int32, (256, 128), 1) < 64
    n_all = normed[...]
    keys = jnp.dot(n_all, wqkv[1], preferred_element_type=F32)
    values = jnp.dot(n_all, wqkv[2], preferred_element_type=F32)
    for g in range(2):
        kg, vg = keys[:, g * 128 : g * 128 + 128], values[:, g * 128 : g * 128 + 128]
        kv_out[2 * g] = jnp.where(low, kg, pltpu.roll(vg, 64, 1)).astype(BF)
        kv_out[2 * g + 1] = jnp.where(low, pltpu.roll(kg, 64, 1), vg).astype(BF)
    query = jnp.dot(n_all, wqkv[0], preferred_element_type=F32)
    low_half = low[:128]
    for g in range(2):
        qa, qb = query[:128, g * 128 : g * 128 + 128], query[128:, g * 128 : g * 128 + 128]
        q_out[2 * g] = jnp.where(low_half, qa, pltpu.roll(qb, 64, 1)).astype(BF)
        q_out[2 * g + 1] = jnp.where(low_half, pltpu.roll(qa, 64, 1), qb).astype(BF)
    for dz in (1, 3, 2):
        head = lax.rem(zl + dz, 4)
        remote(
            kv_out.at[head], kv.at[0, 4 - dz], a_send.at[0], a_recv.at[4 - dz], at(0, dz, 0, 0, 0)
        ).start()
    for dx in (1, 3):
        remote(
            kv_out.at[zl], kv.at[1 if dx == 1 else 2, 0], b_send.at[0],
            b_recv.at[1 if dx == 1 else 2, 0], at(0, 0, dx, 0, 0),
        ).start()
    for dz in (1, 3, 2):
        head = lax.rem(zl + dz, 4)
        remote(
            q_out.at[head], q_in.at[4 - dz], a_send.at[1], q_recv.at[4 - dz], at(0, dz, 0, 0, 0)
        ).start()
    kv[0, 0] = kv_out[zl]

    def unpack(k, packed):
        packed = packed.astype(F32)
        qpad[k, :128] = jnp.where(low_half, packed, 0.0).astype(BF)
        qpad[k, 128:] = jnp.where(low_half, pltpu.roll(packed, 64, 1), 0.0).astype(BF)

    unpack(0, q_out[zl])
    out.finish_x()
    for s in (1, 3, 2):
        arrived(kv.at[0, s], a_recv.at[s])
        for dx in (1, 3):
            slot = 1 if dx == 1 else 2
            remote(
                kv.at[0, s], kv.at[slot, s], b_send.at[0], b_recv.at[slot, s], at(0, 0, dx, 0, 0)
            ).start()
    for s in (1, 3, 2):
        arrived(q_in.at[s], q_recv.at[s])
        unpack(s, q_in[s])

    def score(k, b):
        rows = kv[k].reshape(1024, 128)
        s = lax.dot_general(
            qpad[b], rows, (((1,), (1,)), ((), ())), preferred_element_type=F32
        )
        return rows, s, jnp.max(s, axis=1, keepdims=True)

    def first_block(b, carry):
        rows, s, top = score(0, b)
        w = jnp.exp2(s * SCALE - top * SCALE)
        high[b] = jnp.broadcast_to(top, (256, 128))
        total[b] = jnp.broadcast_to(jnp.sum(w, axis=1, keepdims=True), (256, 128))
        summed[b] = jnp.dot(w.astype(BF), rows, preferred_element_type=F32)
        return carry

    def next_block(k, b):
        rows, s, top = score(k, b)
        before = high[b]
        now = jnp.maximum(before, top)
        fade = jnp.exp2((before - now) * SCALE)
        w = jnp.exp2(s * SCALE - now[:, :1] * SCALE)
        sums = total[b] * fade + jnp.sum(w, axis=1, keepdims=True)
        acc = summed[b] * fade + jnp.dot(w.astype(BF), rows, preferred_element_type=F32)
        return now, sums, acc

    def later_block(k):
        def go(b, carry):
            high[b], total[b], summed[b] = next_block(k, b)
            return carry

        return go

    def relay(slot, s):
        arrived(kv.at[slot, s], b_recv.at[slot, s])
        remote(
            kv.at[slot, s], kv.at[3, s], b_send.at[0], b_recv.at[3, s], at(0, 0, 1 if slot == 1 else 3, 0, 0)
        ).start()

    relay(1, 0)
    relay(2, 1)
    lax.fori_loop(0, 4, first_block, 0)
    relay(2, 3)
    relay(1, 2)
    for s in (1, 3):
        arrived(kv.at[1, s], b_recv.at[1, s])
    lax.fori_loop(0, 4, later_block(1), 0)
    for s in (0, 2):
        arrived(kv.at[2, s], b_recv.at[2, s])
    lax.fori_loop(0, 4, later_block(2), 0)
    for s in range(4):
        arrived(kv.at[3, s], b_recv.at[3, s])
    low64 = low[:64]
    head_here = mp * 4 + zl
    for b in range(4):
        now, sums, acc = next_block(3, b)
        rows = acc / sums
        for half in range(2):
            top_rows = rows[half * 128 : half * 128 + 64]
            low_rows = rows[half * 128 + 64 : half * 128 + 128]
            o_out[b, half] = jnp.where(low64, pltpu.roll(top_rows, 64, 1), low_rows).astype(BF)
        for dh in range(2):
            for dc in range(2):
                if b == 0 and dh == 0 and dc == 0:
                    continue
                half = lax.rem(core + dc, 2)
                remote(
                    o_out.at[b, half], ctx.at[head_here], c_send.at[0], c_recv.at[0], at(0, b, 0, dh, dc)
                ).start()
    ctx[head_here] = o_out[0, core]
    out.local().wait()
    out.wait_all()
    arrived(ctx.at[pl.ds(0, 15)], c_recv.at[0])

    pieces = []
    for g in range(8):
        a, b = ctx[2 * g].astype(F32), ctx[2 * g + 1].astype(F32)
        pieces.append(
            jnp.concatenate(
                [
                    jnp.where(low64, a, pltpu.roll(b, 64, 1)),
                    jnp.where(low64, pltpu.roll(a, 64, 1), b),
                ],
                axis=0,
            ).astype(BF)
        )
    context = jnp.concatenate(pieces, axis=1)
    mine = pl.ds(pl.multiple_of(core * 128, 128), 128)
    h = hidden[mine] + jnp.dot(context, wout[...], preferred_element_type=F32)
    final[mine] = norm_rows(h, gain_out_ref[...]).astype(BF)
    send_final = remote(final.at[mine], final.at[mine], f_send.at[0], f_recv.at[0], at(0, 0, 0, 0, 1))
    send_final.start()

    def finish(block):
        rows = final[block]
        tops = []
        for q in range(4):
            part = lax.dot_general(
                rows, table[q * 256 : q * 256 + 256], (((1,), (1,)), ((), ())), preferred_element_type=F32
            )
            logits[q, block] = part
            tops.append(jnp.max(part, axis=1, keepdims=True))
        top = jnp.maximum(jnp.maximum(tops[0], tops[1]), jnp.maximum(tops[2], tops[3]))
        sums = jnp.zeros_like(top)
        for q in range(4):
            sums = sums + jnp.sum(jnp.exp(logits[q, block] - top), axis=1, keepdims=True)
        lse = top + jnp.log(sums)
        logp_ref[0, block] = (logits[mp, block] - lse).astype(BF)
        qpad_conf = jnp.exp(top - lse)
        high[0, block] = jnp.broadcast_to(qpad_conf, (128, 128))

    finish(mine)
    other = pl.ds(pl.multiple_of((1 - core) * 128, 128), 128)
    arrived(final.at[other], f_recv.at[0])
    finish(other)
    conf = high[0][:, :1]
    w = weight[...][:, :1]
    conf_sum = jnp.sum(conf * w, axis=0, keepdims=True)
    count = jnp.sum(w, axis=0, keepdims=True)
    lane8 = lax.broadcasted_iota(jnp.int32, (8, 128), 1)
    tile = jnp.where(lane8 == 0, conf_sum, jnp.where(lane8 == 1, count, 0.0))
    stat_out[...] = tile
    stat_in[frame] = tile
    conf_ref[...] = jnp.sum(jnp.where(row == lane, conf, 0.0), axis=0, keepdims=True)
    for dz in range(4):
        for dx in range(4):
            if dz or dx:
                remote(
                    stat_out, stat_in.at[frame], s_send.at[0], s_recv.at[0], at(0, dz, dx, 0, 0)
                ).start()
    tab.wait_sent()
    out.wait_sent()
    left(kv_out.at[pl.ds(0, 3)], a_send.at[0])
    left(q_out.at[pl.ds(0, 3)], a_send.at[1])
    left(kv.at[pl.ds(0, 3)], b_send.at[0])
    left(ctx.at[pl.ds(0, 15)], c_send.at[0])
    send_final.wait_send()
    arrived(stat_in.at[pl.ds(0, 15)], s_recv.at[0])
    left(stat_in.at[pl.ds(0, 15)], s_send.at[0])
    sums = stat_in[0]
    for k in range(1, 16):
        sums = sums + stat_in[k]
    sums = sums[:1]
    lane1 = lane8[:1]
    all_conf = jnp.sum(jnp.where(lane1 == 0, sums, 0.0), axis=1, keepdims=True)
    all_count = jnp.sum(jnp.where(lane1 == 1, sums, 0.0), axis=1, keepdims=True)
    stats_ref[...] = jnp.where(lane1 == 0, all_conf / all_count, jnp.log(all_count / 4096.0))


def body(token_ids, remask, position_embed, mask_embed, table, gain_in, gain_out, w_qkv, w_out):
    vmem = pl.BlockSpec(memory_space=pltpu.VMEM)
    hbm = pl.BlockSpec(memory_space=pl.ANY)
    dma = pltpu.SemaphoreType.DMA
    spread_sems = [dma((5,)), dma, dma((8,)), dma((4,)), dma((2,))]
    log_probs, confidence, stats = pl.pallas_call(
        kernel,
        out_shape=(
            jax.ShapeDtypeStruct((1, 256, 256), BF),
            jax.ShapeDtypeStruct((1, 256), F32),
            jax.ShapeDtypeStruct((1, 128), F32),
        ),
        in_specs=[vmem] * 5 + [hbm] * 4,
        out_specs=(vmem, vmem, vmem),
        scratch_shapes=[
            pltpu.VMEM((1024, 1024), BF),
            pltpu.VMEM((1024, 1024), BF),
            pltpu.VMEM((3, 1024, 256), BF),
            pltpu.VMEM((256, 1024), BF),
            pltpu.VMEM((256, 1024), F32),
            pltpu.VMEM((256, 1024), BF),
            pltpu.VMEM((4, 256, 128), BF),
            pltpu.VMEM((4, 128, 128), BF),
            pltpu.VMEM((4, 4, 256, 128), BF),
            pltpu.VMEM((4, 128, 128), BF),
            pltpu.VMEM((4, 256, 128), BF),
            pltpu.VMEM((4, 256, 128), F32),
            pltpu.VMEM((4, 256, 128), F32),
            pltpu.VMEM((4, 256, 128), F32),
            pltpu.VMEM((4, 2, 64, 128), BF),
            pltpu.VMEM((16, 64, 128), BF),
            pltpu.VMEM((256, 1024), BF),
            pltpu.VMEM((4, 256, 256), F32),
            pltpu.VMEM((256, 128), F32),
            pltpu.VMEM((8, 128), F32),
            pltpu.VMEM((16, 8, 128), F32),
            dma((2,)),
            *spread_sems,
            *spread_sems,
            dma((2,)),
            dma((4,)),
            dma((4,)),
            dma((1,)),
            dma((4, 4)),
            dma((1,)),
            dma((1,)),
            dma((1,)),
            dma((1,)),
            dma((1,)),
            dma((1,)),
        ],
        compiler_params=pltpu.CompilerParams(
            collective_id=0, has_side_effects=True, vmem_limit_bytes=60 * 1024 * 1024
        ),
        name="predict",
    )(
        token_ids,
        remask,
        mask_embed.reshape(1, -1),
        gain_in.reshape(1, -1),
        gain_out.reshape(1, -1),
        table,
        w_qkv,
        w_out,
        position_embed,
    )
    return log_probs, confidence, stats[0, :2]


def solution(mesh):
    finer = Mesh(mesh.devices.reshape(8, 4, 4, 2, 2), AXES)
    frames = ("clip", "zl", "x")
    tm = ("zl", "x")
    mp = ("zh", "core")
    in_specs = (
        P(frames, None),
        P(frames, None),
        P(tm, None, None),
        P(),
        P(mp, None),
        P(),
        P(),
        P(None, None, mp),
        P(mp, None),
    )
    out_specs = (P(frames, None, mp), P(frames, None), P("clip"))
    return jax.shard_map(body, mesh=finer, in_specs=in_specs, out_specs=out_specs, check_vma=False)
```

time: 302 us -> 79.7 us (0.26)
  blocking collectives: 114 us -> 0 us
  waiting for transfers between devices: 73.8 us -> 0 us
  Pallas kernels: 0 us -> 73.6 us
  matrix products: 37.5 us -> 0 us
  other arithmetic: 24.3 us -> 0 us
  starting transfers between devices: 21.6 us -> 0 us
  between operations: 16.4 us -> 0.64 us
  local copies, waits for them, and re-layouts: 12.3 us -> 5.24 us
    all_to_all x4 -> x0, blocking collectives: 81.7 us -> none  [the longest x3 51.1 us: sent_to_all(): lax.all_to_all(jnp.broadcast_to(array[None], (size, *array.shape)), axis,...]
    pallas_call x0 -> x1, Pallas kernels: none -> 73.6 us  [body(): pl.pallas_call(kernel, out_shape=(jax.ShapeDtypeStruct((1, 256, 256), BF)...]
    all_gather x2 -> x0, waiting for transfers between devices: 55.9 us -> none  [gather_axes(): array = lax.all_gather(array, axis, axis=dim, tiled=True)]
    dot_general x20 -> x0, matrix products: 37.5 us -> none  [the longest x8 22.2 us: absorb_block(): jnp.einsum('qhd,khd->hqk', query, key_block, preferred_element_type=jnp.f...]
    all_gather x2 -> x0, blocking collectives: 32.7 us -> none  [gather_axes(): array = lax.all_gather(array, axis, axis=dim, tiled=True)]
    all_to_all x2 -> x0, starting transfers between devices: 21.6 us -> none  [the longest x1 11.8 us: sum_at_owner(): blocks = lax.all_to_all(split_up(array, dim, size), axis, 0, 0, tiled=True)]
    reduce_sum x17 -> x0, other arithmetic: 20.2 us -> none  [the longest x8 16.8 us: absorb_block(): totals = totals * fade + jnp.sum(weights, axis=-1)]
    all_to_all x2 -> x0, waiting for transfers between devices: 17.9 us -> none  [the longest x1 11.9 us: sum_at_owner(): blocks = lax.all_to_all(split_up(array, dim, size), axis, 0, 0, tiled=True)]
  transfers between devices with their start and end apart: 4 -> 0, of which waited for: 4 -> 0; matrix products, arithmetic and copies ran while one was open for 2% -> 0% of each run, Pallas kernels for 0% -> 0%
where the time goes in v1:
time: 79.7 us; the launch traced here: 79.5 us
  Pallas kernels  73.6 us (92%)
  local copies, waits for them, and re-layouts  5.24 us (7%)
    pallas_call x1, Pallas kernels, body(): pl.pallas_call(kernel, out_shape=(jax.ShapeDtypeStruct((1, 256, 256), BF)...  73.6 us
    unnamed x2, local copies, waits for them, and re-layouts  2.79 us

profile of v1, /device:TPU:1, one launch (start us, length us, event | category | flops | bytes accessed | tf_op | source)
XLA Modules:
  0.0 79.5 jit_solution(11311243491511149393)
XLA Ops:
  0.6 1.3 %reshape.15.mask_embed_ref = bf16[1,1024]{1,0:T(2,128)(2,1)} reshape(bf16[1024]{0:T(1024)(128)(2,1)} %param.12) | data formatting | bytes 4096 | tf_op jit(solution)/shard_map/reshape | solution.py:452
  1.9 73.6 %predict.1 = (bf16[1,256,256]{2,1,0:T(8,128)(2,1)}, f32[1,256]{1,0:T(1,128)}, f32[1,128]{1,0:T(1,128)}) custom-call(s32[1,256]{1,0:T(1,128)} %ids_ref.1, s32[1,256]{1,0:T(1,128)} %remask_ref.1, bf16[1,1024]{1,0:T(2,128)(2,1)} %reshape.15.mask_embed_ref, f32[1,1024]{1,0:T(1,128)} %bitcast.4, f32[1,1024]{1,0:T(1,128)} %bitcast.5, bf16[256,1024]{1,0:T(8,128)(2,1)} %table_hbm.1, ...), custom_call_target="tpu_custom_call" | custom-call | tf_op jit(solution)/shard_map/predict/pallas_call | solution.py:399
  75.5 1.2 %slice_bitcast_fusion = f32[2]{0:T(128)} fusion(f32[1,128]{1,0:T(1,128)} %get-tuple-element.8), kind=kLoop, calls=%fused_computation | loop fusion | bytes 16 | tf_op jit(solution)/shard_map/squeeze | solution.py:460
  76.7 1.6 %copy.14 = bf16[1,256,256]{2,1,0:T(8,128)(2,1)} copy(bf16[1,256,256]{2,1,0:T(8,128)(2,1)} %get-tuple-element.12) | data formatting | bytes 262144
  78.2 1.2 %copy.15 = f32[1,256]{1,0:T(1,128)} copy(f32[1,256]{1,0:T(1,128)} %get-tuple-element.13) | data formatting | bytes 2048

commit v2 on v1

--- a/solution.py
+++ b/solution.py
@@ -74,9 +74,8 @@
         return pltpu.make_async_copy(self.hbm, self.full.at[quarter], self.ssem.at[4])
 
     def start_z(self):
-        src = self.hbm.at[pl.ds(pl.multiple_of(self.x * 64, 64), 64), self.cols(self.y)]
-        dst = self.full.at[self.rows(self.own, self.x), self.cols(self.y)]
-        remote(src, dst, self.ssem.at[0], self.zsem, mirror()).start()
+        piece = self.full.at[self.rows(self.own, self.x), self.cols(self.y)]
+        remote(piece, piece, self.ssem.at[0], self.zsem, mirror()).start()
 
     def start_own_quarter(self):
         quarter = pl.ds(pl.multiple_of(self.own * 256, 256), 256)
@@ -113,6 +112,35 @@
             x = lax.rem(self.x - dx + 4, 4)
             arrived(self.full.at[self.rows(self.got, x)], self.xsem.at[dx])
             self.hand_over(x)
+
+    def start_x_first(self):
+        piece = self.full.at[self.rows(self.got, self.x), self.cols(self.y)]
+        arrived(piece, self.zsem)
+        for dx in (2, 1, 3):
+            remote(piece, piece, self.ssem.at[2], self.xsem.at[dx], at(0, 0, dx, 0, 0)).start()
+
+    def strip(self, y):
+        return self.full.at[pl.ds(pl.multiple_of(self.got * 256, 256), 256), self.cols(y)]
+
+    def start_y_second(self):
+        for dx in (1, 3, 2):
+            x = lax.rem(self.x - dx + 4, 4)
+            arrived(self.full.at[self.rows(self.got, x), self.cols(self.y)], self.xsem.at[dx])
+        strip = self.strip(self.y)
+        for dy in (4, 3, 5, 2, 6, 1, 7):
+            remote(strip, strip, self.ssem.at[1], self.ysem.at[dy], at(dy, 0, 0, 0, 0)).start()
+
+    def finish_y_second(self):
+        for dy in (1, 7, 2, 6, 3, 5, 4):
+            arrived(self.strip(lax.rem(self.y - dy + 8, 8)), self.ysem.at[dy])
+        quarter = self.full.at[pl.ds(pl.multiple_of(self.got * 256, 256), 256)]
+        remote(quarter, quarter, self.ssem.at[3], self.dsem.at[1], at(0, 0, 0, 0, 1)).start()
+
+    def wait_sent_x_first(self):
+        left(self.full.at[pl.ds(0, 64), pl.ds(0, 128)], self.ssem.at[0])
+        left(self.full.at[pl.ds(0, 256), pl.ds(0, 896)], self.ssem.at[1])
+        left(self.full.at[pl.ds(0, 64), pl.ds(0, 384)], self.ssem.at[2])
+        left(self.full.at[pl.ds(0, 512)], self.ssem.at[3])
 
     def wait_all(self):
         quarter = self.full.at[pl.ds(0, 256)]
@@ -148,7 +176,7 @@
         place = lax.rem(zh * 8 + zl * 2 + core + k, 16)
         peers.append((y, lax.rem(place // 2, 4), x, place // 8, lax.rem(place, 2)))
     peers += [at(k, 0, 0, 0, 0) for k in range(1, 8)]
-    peers += [at(0, dz, dx, 0, 0) for dx in range(1, 4) for dz in range(4)]
+    peers += [at(0, dz, dx, 0, dc) for dx in range(1, 4) for dz in range(4) for dc in range(2)]
     for peer in peers:
         pl.semaphore_signal(barrier, inc=1, device_id=peer, device_id_type=MESH)
     tab.local().start()
@@ -163,37 +191,40 @@
         jnp.where(row == lane, ids_ref[...].astype(F32), 0.0), axis=1, keepdims=True
     )
     weight[...] = jnp.broadcast_to(masked, (256, 128))
-    entry = lax.broadcasted_iota(jnp.int32, (256, 1024), 1).astype(F32)
-    onehot = jnp.where(entry == jnp.where(masked > 0.5, -1.0, ids_col), 1.0, 0.0).astype(BF)
-
+    ids_col = jnp.where(masked > 0.5, -1.0, ids_col)
+    entry = lax.broadcasted_iota(jnp.int32, (256, 512), 1)
+    mask_row = mask_embed_ref[...].astype(F32).reshape(1, 1024)
+
+    def looked_up(half):
+        onehot = jnp.where((entry + half * 512).astype(F32) == ids_col, 1.0, 0.0).astype(BF)
+        rows = table[pl.ds(pl.multiple_of(half * 512, 512), 512)]
+        return jnp.dot(onehot, rows, preferred_element_type=F32)
+
+    load_pos.wait()
+    for k in range(4):
+        block = slice(k * 64, k * 64 + 64)
+        hidden[block] = pos[block].astype(F32) + jnp.where(masked[block] > 0.5, mask_row, 0.0)
+    tab.local().wait()
+    out.local().wait()
     pl.semaphore_wait(barrier, len(peers))
     tab.start_z()
+    tab.start_own_quarter()
     out.start_z()
-    tab.start_own_quarter()
     tab.start_y()
-    out.start_y()
+    arrived(table.at[pl.ds(0, 256)], tab.dsem.at[0])
+    hidden[...] += looked_up(zh)
     tab.start_x()
+    out.start_x_first()
     tab.finish_x()
+    out.start_y_second()
     out.start_own_quarter()
-    out.start_x()
-    tab.local().wait()
-    load_pos.wait()
     load_qkv.wait()
-    tab.wait_all()
-
-    hidden[...] = jnp.dot(onehot, table[...], preferred_element_type=F32)
-    mask_row = mask_embed_ref[...].astype(F32)
+    arrived(table.at[pl.ds(0, 256)], tab.dsem.at[1])
+    hidden[...] += looked_up(1 - zh)
     gain_in = gain_in_ref[...]
-
-    def first_norm(k, carry):
-        block = pl.ds(pl.multiple_of(k * 64, 64), 64)
-        h = hidden[block] + jnp.where(weight[block][:, :1] > 0.5, mask_row, 0.0)
-        h = h + pos[block].astype(F32)
-        hidden[block] = h
-        normed[block] = norm_rows(h, gain_in).astype(BF)
-        return carry
-
-    lax.fori_loop(0, 4, first_norm, 0)
+    for k in range(4):
+        block = slice(k * 64, k * 64 + 64)
+        normed[block] = norm_rows(hidden[block], gain_in).astype(BF)
     low = lax.broadcasted_iota(jnp.int32, (256, 128), 1) < 64
     n_all = normed[...]
     keys = jnp.dot(n_all, wqkv[1], preferred_element_type=F32)
@@ -208,21 +239,22 @@
         qa, qb = query[:128, g * 128 : g * 128 + 128], query[128:, g * 128 : g * 128 + 128]
         q_out[2 * g] = jnp.where(low_half, qa, pltpu.roll(qb, 64, 1)).astype(BF)
         q_out[2 * g + 1] = jnp.where(low_half, pltpu.roll(qa, 64, 1), qb).astype(BF)
-    for dz in (1, 3, 2):
-        head = lax.rem(zl + dz, 4)
-        remote(
-            kv_out.at[head], kv.at[0, 4 - dz], a_send.at[0], a_recv.at[4 - dz], at(0, dz, 0, 0, 0)
-        ).start()
-    for dx in (1, 3):
-        remote(
-            kv_out.at[zl], kv.at[1 if dx == 1 else 2, 0], b_send.at[0],
-            b_recv.at[1 if dx == 1 else 2, 0], at(0, 0, dx, 0, 0),
-        ).start()
+    def pass_on(block, s):
+        for dx in (1, 3, 2):
+            slot = (0, 1, 3, 2)[dx]
+            remote(block, kv.at[s, slot], b_send.at[0], b_recv.at[s, slot], at(0, 0, dx, 0, 0)).start()
+
+    pass_on(kv_out.at[zl], 0)
     for dz in (1, 3, 2):
         head = lax.rem(zl + dz, 4)
         remote(
             q_out.at[head], q_in.at[4 - dz], a_send.at[1], q_recv.at[4 - dz], at(0, dz, 0, 0, 0)
         ).start()
+    for dz in (3, 1, 2):
+        head = lax.rem(zl + dz, 4)
+        remote(
+            kv_out.at[head], kv.at[4 - dz, 0], a_send.at[0], a_recv.at[4 - dz], at(0, dz, 0, 0, 0)
+        ).start()
     kv[0, 0] = kv_out[zl]
 
     def unpack(k, packed):
@@ -231,91 +263,78 @@
         qpad[k, 128:] = jnp.where(low_half, pltpu.roll(packed, 64, 1), 0.0).astype(BF)
 
     unpack(0, q_out[zl])
-    out.finish_x()
-    for s in (1, 3, 2):
-        arrived(kv.at[0, s], a_recv.at[s])
-        for dx in (1, 3):
-            slot = 1 if dx == 1 else 2
-            remote(
-                kv.at[0, s], kv.at[slot, s], b_send.at[0], b_recv.at[slot, s], at(0, 0, dx, 0, 0)
-            ).start()
-    for s in (1, 3, 2):
-        arrived(q_in.at[s], q_recv.at[s])
-        unpack(s, q_in[s])
-
-    def score(k, b):
-        rows = kv[k].reshape(1024, 128)
-        s = lax.dot_general(
-            qpad[b], rows, (((1,), (1,)), ((), ())), preferred_element_type=F32
+    low64 = low[:64]
+    head_here = mp * 4 + zl
+
+    def ready(s, b):
+        if s == 0:
+            if b == 0:
+                for slot in (1, 2, 3):
+                    arrived(kv.at[0, slot], b_recv.at[0, slot])
+            else:
+                arrived(q_in.at[b], q_recv.at[b])
+                unpack(b, q_in[b])
+        elif b == 0:
+            for slot in (1, 2, 3):
+                arrived(kv.at[s, slot], b_recv.at[s, slot])
+
+    def score(s, b):
+        return lax.dot_general(
+            qpad[b], kv[s].reshape(1024, 128), (((1,), (1,)), ((), ())), preferred_element_type=F32
         )
-        return rows, s, jnp.max(s, axis=1, keepdims=True)
-
-    def first_block(b, carry):
-        rows, s, top = score(0, b)
-        w = jnp.exp2(s * SCALE - top * SCALE)
-        high[b] = jnp.broadcast_to(top, (256, 128))
-        total[b] = jnp.broadcast_to(jnp.sum(w, axis=1, keepdims=True), (256, 128))
-        summed[b] = jnp.dot(w.astype(BF), rows, preferred_element_type=F32)
-        return carry
-
-    def next_block(k, b):
-        rows, s, top = score(k, b)
+
+    def absorb(s, b, scores):
+        rows = kv[s].reshape(1024, 128)
+        top = jnp.max(scores, axis=1, keepdims=True)
+        if s == 0:
+            w = jnp.exp2(scores * SCALE - top * SCALE)
+            high[b] = jnp.broadcast_to(top, (256, 128))
+            total[b] = jnp.broadcast_to(jnp.sum(w, axis=1, keepdims=True), (256, 128))
+            summed[b] = jnp.dot(w.astype(BF), rows, preferred_element_type=F32)
+            return
         before = high[b]
         now = jnp.maximum(before, top)
         fade = jnp.exp2((before - now) * SCALE)
-        w = jnp.exp2(s * SCALE - now[:, :1] * SCALE)
+        w = jnp.exp2(scores * SCALE - now[:, :1] * SCALE)
         sums = total[b] * fade + jnp.sum(w, axis=1, keepdims=True)
         acc = summed[b] * fade + jnp.dot(w.astype(BF), rows, preferred_element_type=F32)
-        return now, sums, acc
-
-    def later_block(k):
-        def go(b, carry):
-            high[b], total[b], summed[b] = next_block(k, b)
-            return carry
-
-        return go
-
-    def relay(slot, s):
-        arrived(kv.at[slot, s], b_recv.at[slot, s])
-        remote(
-            kv.at[slot, s], kv.at[3, s], b_send.at[0], b_recv.at[3, s], at(0, 0, 1 if slot == 1 else 3, 0, 0)
-        ).start()
-
-    relay(1, 0)
-    relay(2, 1)
-    lax.fori_loop(0, 4, first_block, 0)
-    relay(2, 3)
-    relay(1, 2)
-    for s in (1, 3):
-        arrived(kv.at[1, s], b_recv.at[1, s])
-    lax.fori_loop(0, 4, later_block(1), 0)
-    for s in (0, 2):
-        arrived(kv.at[2, s], b_recv.at[2, s])
-    lax.fori_loop(0, 4, later_block(2), 0)
-    for s in range(4):
-        arrived(kv.at[3, s], b_recv.at[3, s])
-    low64 = low[:64]
-    head_here = mp * 4 + zl
-    for b in range(4):
-        now, sums, acc = next_block(3, b)
+        if s != 2:
+            high[b], total[b], summed[b] = now, sums, acc
+            return
         rows = acc / sums
         for half in range(2):
             top_rows = rows[half * 128 : half * 128 + 64]
             low_rows = rows[half * 128 + 64 : half * 128 + 128]
             o_out[b, half] = jnp.where(low64, pltpu.roll(top_rows, 64, 1), low_rows).astype(BF)
-        for dh in range(2):
-            for dc in range(2):
+
+    def send_context(b):
+        for dh in (1, 0):
+            for dc in (0, 1):
                 if b == 0 and dh == 0 and dc == 0:
                     continue
                 half = lax.rem(core + dc, 2)
                 remote(
                     o_out.at[b, half], ctx.at[head_here], c_send.at[0], c_recv.at[0], at(0, b, 0, dh, dc)
                 ).start()
+
+    steps = [(s, b) for s in (0, 1, 3, 2) for b in (0, 1, 3, 2)]
+    ready(0, 0)
+    scores = score(0, 0)
+    for i, (s, b) in enumerate(steps):
+        for arriving in {(0, 2): (1, 3), (1, 1): (2,)}.get((s, b), ()):
+            arrived(kv.at[arriving, 0], a_recv.at[arriving])
+            pass_on(kv.at[arriving, 0], arriving)
+        if i + 1 < len(steps):
+            ready(*steps[i + 1])
+            following = score(*steps[i + 1])
+        absorb(s, b, scores)
+        if s == 2:
+            send_context(b)
+        scores = following
+    out.finish_y_second()
     ctx[head_here] = o_out[0, core]
-    out.local().wait()
     out.wait_all()
     arrived(ctx.at[pl.ds(0, 15)], c_recv.at[0])
-
     pieces = []
     for g in range(8):
         a, b = ctx[2 * g].astype(F32), ctx[2 * g + 1].astype(F32)
@@ -350,45 +369,53 @@
             sums = sums + jnp.sum(jnp.exp(logits[q, block] - top), axis=1, keepdims=True)
         lse = top + jnp.log(sums)
         logp_ref[0, block] = (logits[mp, block] - lse).astype(BF)
-        qpad_conf = jnp.exp(top - lse)
-        high[0, block] = jnp.broadcast_to(qpad_conf, (128, 128))
-
-    finish(mine)
+        conf = jnp.exp(top - lse)
+        high[0, block] = jnp.broadcast_to(conf, (128, 128))
+        return conf
+
+    conf = finish(mine)
+    w = weight[mine][:, :1]
+    lane8 = lax.broadcasted_iota(jnp.int32, (8, 128), 1)
+    conf_sum = jnp.sum(conf * w, axis=0, keepdims=True)
+    count = jnp.sum(w, axis=0, keepdims=True)
+    tile = jnp.where(lane8 == 0, conf_sum, jnp.where(lane8 == 1, count, 0.0))
+    place = frame * 2 + core
+    stat_out[...] = tile
+    stat_in[place] = tile
+    for dz in (2, 3, 1, 0):
+        for dx in (2, 3, 1, 0):
+            for dc in range(2):
+                if dz or dx or dc:
+                    remote(
+                        stat_out, stat_in.at[place], s_send.at[0], s_recv.at[0], at(0, dz, dx, 0, dc)
+                    ).start()
     other = pl.ds(pl.multiple_of((1 - core) * 128, 128), 128)
     arrived(final.at[other], f_recv.at[0])
     finish(other)
-    conf = high[0][:, :1]
-    w = weight[...][:, :1]
-    conf_sum = jnp.sum(conf * w, axis=0, keepdims=True)
-    count = jnp.sum(w, axis=0, keepdims=True)
-    lane8 = lax.broadcasted_iota(jnp.int32, (8, 128), 1)
-    tile = jnp.where(lane8 == 0, conf_sum, jnp.where(lane8 == 1, count, 0.0))
-    stat_out[...] = tile
-    stat_in[frame] = tile
-    conf_ref[...] = jnp.sum(jnp.where(row == lane, conf, 0.0), axis=0, keepdims=True)
-    for dz in range(4):
-        for dx in range(4):
-            if dz or dx:
-                remote(
-                    stat_out, stat_in.at[frame], s_send.at[0], s_recv.at[0], at(0, dz, dx, 0, 0)
-                ).start()
+    conf_ref[...] = jnp.sum(jnp.where(row == lane, high[0][:, :1], 0.0), axis=0, keepdims=True)
     tab.wait_sent()
-    out.wait_sent()
+    out.wait_sent_x_first()
     left(kv_out.at[pl.ds(0, 3)], a_send.at[0])
     left(q_out.at[pl.ds(0, 3)], a_send.at[1])
     left(kv.at[pl.ds(0, 3)], b_send.at[0])
     left(ctx.at[pl.ds(0, 15)], c_send.at[0])
     send_final.wait_send()
-    arrived(stat_in.at[pl.ds(0, 15)], s_recv.at[0])
-    left(stat_in.at[pl.ds(0, 15)], s_send.at[0])
+    arrived(stat_in.at[pl.ds(0, 31)], s_recv.at[0])
+    left(stat_in.at[pl.ds(0, 31)], s_send.at[0])
     sums = stat_in[0]
-    for k in range(1, 16):
+    for k in range(1, 32):
         sums = sums + stat_in[k]
     sums = sums[:1]
     lane1 = lane8[:1]
     all_conf = jnp.sum(jnp.where(lane1 == 0, sums, 0.0), axis=1, keepdims=True)
     all_count = jnp.sum(jnp.where(lane1 == 1, sums, 0.0), axis=1, keepdims=True)
     stats_ref[...] = jnp.where(lane1 == 0, all_conf / all_count, jnp.log(all_count / 4096.0))
+
+
+def write_out(logp, conf, stats, logp_out, conf_out, stats_out):
+    logp_out[...] = logp[...]
+    conf_out[...] = conf[...]
+    stats_out[...] = stats[:, :2]
 
 
 def body(token_ids, remask, position_embed, mask_embed, table, gain_in, gain_out, w_qkv, w_out):
@@ -426,7 +453,7 @@
             pltpu.VMEM((4, 256, 256), F32),
             pltpu.VMEM((256, 128), F32),
             pltpu.VMEM((8, 128), F32),
-            pltpu.VMEM((16, 8, 128), F32),
+            pltpu.VMEM((32, 8, 128), F32),
             dma((2,)),
             *spread_sems,
             *spread_sems,
@@ -449,7 +476,7 @@
     )(
         token_ids,
         remask,
-        mask_embed.reshape(1, -1),
+        mask_embed,
         gain_in.reshape(1, -1),
         gain_out.reshape(1, -1),
         table,
@@ -457,7 +484,18 @@
         w_out,
         position_embed,
     )
-    return log_probs, confidence, stats[0, :2]
+    log_probs, confidence, stats = pl.pallas_call(
+        write_out,
+        out_shape=(
+            jax.ShapeDtypeStruct((1, 256, 256), BF),
+            jax.ShapeDtypeStruct((1, 256), F32),
+            jax.ShapeDtypeStruct((1, 2), F32),
+        ),
+        in_specs=[vmem] * 3,
+        out_specs=(vmem, vmem, vmem),
+        name="write_out",
+    )(log_probs, confidence, stats)
+    return log_probs, confidence, stats.reshape(2)
 
 
 def solution(mesh):

time: 79.7 us -> 72 us (0.903)
  local copies, waits for them, and re-layouts: 5.24 us -> 0 us
  Pallas kernels: 73.6 us -> 71.1 us
    pallas_call x1, Pallas kernels: 73.6 us -> 69.5 us  [body(): pl.pallas_call(kernel, out_shape=(jax.ShapeDtypeStruct((1, 256, 256), BF)...]
    unnamed x2 -> x0, local copies, waits for them, and re-layouts: 2.79 us -> none
    pallas_call x0 -> x1, Pallas kernels: none -> 1.58 us  [body(): pl.pallas_call(write_out, out_shape=(jax.ShapeDtypeStruct((1, 256, 256),...]
    reshape x1 -> x0, local copies, waits for them, and re-layouts: 1.28 us -> none  [body(): mask_embed.reshape(1, -1)]
    squeeze x1 -> x0, local copies, waits for them, and re-layouts: 1.16 us -> none  [body(): return (log_probs, confidence, stats[0, :2])]
where the time goes in v2:
time: 72 us; the launch traced here: 71.8 us
  Pallas kernels  71.1 us (99%)
    pallas_call x1, Pallas kernels, body(): pl.pallas_call(kernel, out_shape=(jax.ShapeDtypeStruct((1, 256, 256), BF)...  69.5 us
    pallas_call x1, Pallas kernels, body(): pl.pallas_call(write_out, out_shape=(jax.ShapeDtypeStruct((1, 256, 256),...  1.58 us

profile of v2, /device:TPU:1, one launch (start us, length us, event | category | flops | bytes accessed | tf_op | source)
XLA Modules:
  0.0 71.8 jit_solution(5846662265992287925)
XLA Ops:
  0.6 69.5 %predict.1 = (bf16[1,256,256]{2,1,0:T(8,128)(2,1)}, f32[1,256]{1,0:T(1,128)}, f32[1,128]{1,0:T(1,128)}) custom-call(s32[1,256]{1,0:T(1,128)} %ids_ref.1, s32[1,256]{1,0:T(1,128)} %remask_ref.1, bf16[1024]{0:T(1024)(128)(2,1)} %mask_embed_ref.1, f32[1,1024]{1,0:T(1,128)} %bitcast.3, f32[1,1024]{1,0:T(1,128)} %bitcast.4, bf16[256,1024]{1,0:T(8,128)(2,1)} %table_hbm.1, ...), custom_call_target="tpu_custom_call" | custom-call | tf_op jit(solution)/shard_map/predict/pallas_call | solution.py:426
  70.2 1.6 %write_out.1 = (bf16[1,256,256]{2,1,0:T(8,128)(2,1)}, f32[1,256]{1,0:T(1,128)}, f32[1,2]{1,0:T(1,128)}) custom-call(bf16[1,256,256]{2,1,0:T(8,128)(2,1)} %get-tuple-element.9.logp, f32[1,256]{1,0:T(1,128)} %get-tuple-element.10.conf, f32[1,128]{1,0:T(1,128)} %get-tuple-element.11.stats), custom_call_target="tpu_custom_call" | custom-call | tf_op jit(solution)/shard_map/write_out/pallas_call | solution.py:487

commit v3 on v2

--- a/solution.py
+++ b/solution.py
@@ -55,91 +55,122 @@
 
 
 class Spread:
-    def __init__(self, hbm, full, ssem, zsem, ysem, xsem, dsem):
-        self.hbm, self.full = hbm, full
-        self.ssem, self.zsem, self.ysem, self.xsem, self.dsem = ssem, zsem, ysem, xsem, dsem
+    def __init__(self, hbm, full, first, ssem, zsem, y1sem, x1sem, y2sem, x2sem, dsem):
+        self.hbm, self.full, self.first, self.ssem, self.zsem, self.dsem = hbm, full, first, ssem, zsem, dsem
+        self.y1, self.x1, self.y2, self.x2 = y1sem, x1sem, y2sem, x2sem
         y, zl, x, zh, core = coords()
-        self.y, self.x = y, x
+        self.yq, self.x = lax.rem(y, 4), x
         self.own = zh * 2 + core
         self.got = (1 - zh) * 2 + core
 
+    def quarter(self, k):
+        return pl.ds(pl.multiple_of(k * 256, 256), 256)
+
     def rows(self, quarter, x):
         return pl.ds(pl.multiple_of(quarter * 256 + x * 64, 64), 64)
 
-    def cols(self, y):
-        return pl.ds(pl.multiple_of(y * 128, 128), 128)
+    def cols(self, yq, half):
+        return pl.ds(pl.multiple_of(half * 512 + yq * 128, 128), 128)
+
+    def piece(self, x, yq, half):
+        return self.full.at[self.rows(self.got, x), self.cols(yq, half)]
+
+    def strip(self, yq, half):
+        return self.full.at[self.quarter(self.got), self.cols(yq, half)]
+
+    def block(self, x):
+        return self.full.at[self.rows(self.got, x), pl.ds(0, 512)]
+
+    def y_of(self, dy):
+        return lax.rem(self.yq - dy + 8, 4)
+
+    def x_of(self, dx):
+        return lax.rem(self.x - dx + 4, 4)
 
     def local(self):
-        quarter = pl.ds(pl.multiple_of(self.own * 256, 256), 256)
-        return pltpu.make_async_copy(self.hbm, self.full.at[quarter], self.ssem.at[4])
+        return pltpu.make_async_copy(self.hbm, self.full.at[self.quarter(self.own)], self.ssem.at[4])
+
+    def fetch(self, half):
+        rows = pl.ds(pl.multiple_of(self.x * 64, 64), 64)
+        return pltpu.make_async_copy(
+            self.hbm.at[rows, self.cols(self.yq, half)], self.first.at[half], self.ssem.at[5 + half]
+        )
 
     def start_z(self):
-        piece = self.full.at[self.rows(self.own, self.x), self.cols(self.y)]
-        remote(piece, piece, self.ssem.at[0], self.zsem, mirror()).start()
+        for half in range(2):
+            piece = self.full.at[self.rows(self.own, self.x), self.cols(self.yq, half)]
+            remote(self.first.at[half], piece, self.ssem.at[0], self.zsem.at[half], mirror()).start()
 
     def start_own_quarter(self):
-        quarter = pl.ds(pl.multiple_of(self.own * 256, 256), 256)
-        remote(
-            self.hbm, self.full.at[quarter], self.ssem.at[3], self.dsem.at[0], at(0, 0, 0, 0, 1)
-        ).start()
-
-    def forward_x(self, y):
-        piece = self.full.at[self.rows(self.got, self.x), self.cols(y)]
+        self.hand_over(self.full.at[self.quarter(self.own)], 0)
+
+    def hand_over(self, ref, k):
+        remote(ref, ref, self.ssem.at[3], self.dsem.at[k], at(0, 0, 0, 0, 1)).start()
+
+    def along_y(self, ref, sem, recv):
+        for dy in (2, 1, 7):
+            remote(ref, ref, self.ssem.at[sem], recv.at[dy], at(dy, 0, 0, 0, 0)).start()
+
+    def along_x(self, ref, sem, recv):
+        for dx in (2, 1, 3):
+            remote(ref, ref, self.ssem.at[sem], recv.at[dx], at(0, 0, dx, 0, 0)).start()
+
+    def begin(self):
+        first, second = self.piece(self.x, self.yq, 0), self.piece(self.x, self.yq, 1)
+        arrived(first, self.zsem.at[0])
+        self.along_y(first, 1, self.y1)
+        arrived(second, self.zsem.at[1])
+        self.along_x(second, 1, self.x1)
+        self.along_x(first, 2, self.x2)
+        self.along_y(second, 2, self.y2)
+
+    def forward(self):
+        for dy, dx in ((1, 1), (7, 3), (2, 2)):
+            first = self.piece(self.x, self.y_of(dy), 0)
+            arrived(first, self.y1.at[dy])
+            self.along_x(first, 2, self.x2)
+            second = self.piece(self.x_of(dx), self.yq, 1)
+            arrived(second, self.x1.at[dx])
+            self.along_y(second, 2, self.y2)
+        self.hand_over(self.block(self.x), 1)
+        self.hand_over(self.strip(self.yq, 1), 1)
+
+    def finish(self):
+        for dy, dx in ((1, 1), (7, 3), (2, 2)):
+            block = self.block(self.x_of(dx))
+            arrived(block, self.x2.at[dx])
+            self.hand_over(block, 1)
+            strip = self.strip(self.y_of(dy), 1)
+            arrived(strip, self.y2.at[dy])
+            self.hand_over(strip, 1)
+
+    def wait_sent(self):
+        left(self.full.at[pl.ds(0, 64), pl.ds(0, 256)], self.ssem.at[0])
+        left(self.full.at[pl.ds(0, 64), pl.ds(0, 768)], self.ssem.at[1])
+        left(self.full.at[pl.ds(0, 192)], self.ssem.at[2])
+        left(self.full.at[pl.ds(0, 512)], self.ssem.at[3])
+
+    def begin_slow(self):
+        for half in range(2):
+            piece = self.piece(self.x, self.yq, half)
+            arrived(piece, self.zsem.at[half])
+            self.along_x(piece, 1, self.x1)
+
+    def forward_slow(self):
         for dx in (1, 3, 2):
-            remote(piece, piece, self.ssem.at[2], self.xsem.at[dx], at(0, 0, dx, 0, 0)).start()
-
-    def start_y(self):
-        piece = self.full.at[self.rows(self.got, self.x), self.cols(self.y)]
-        arrived(piece, self.zsem)
-        for dy in (4, 3, 5, 2, 6, 1, 7):
-            remote(piece, piece, self.ssem.at[1], self.ysem.at[dy], at(dy, 0, 0, 0, 0)).start()
-        self.forward_x(self.y)
-
-    def start_x(self):
-        for dy in (1, 7, 2, 6, 3, 5, 4):
-            source = lax.rem(self.y - dy + 8, 8)
-            piece = self.full.at[self.rows(self.got, self.x), self.cols(source)]
-            arrived(piece, self.ysem.at[dy])
-            self.forward_x(source)
-        self.hand_over(self.x)
-
-    def hand_over(self, x):
-        block = self.full.at[self.rows(self.got, x)]
-        remote(block, block, self.ssem.at[3], self.dsem.at[1], at(0, 0, 0, 0, 1)).start()
-
-    def finish_x(self):
-        for dx in (1, 3, 2):
-            x = lax.rem(self.x - dx + 4, 4)
-            arrived(self.full.at[self.rows(self.got, x)], self.xsem.at[dx])
-            self.hand_over(x)
-
-    def start_x_first(self):
-        piece = self.full.at[self.rows(self.got, self.x), self.cols(self.y)]
-        arrived(piece, self.zsem)
-        for dx in (2, 1, 3):
-            remote(piece, piece, self.ssem.at[2], self.xsem.at[dx], at(0, 0, dx, 0, 0)).start()
-
-    def strip(self, y):
-        return self.full.at[pl.ds(pl.multiple_of(self.got * 256, 256), 256), self.cols(y)]
-
-    def start_y_second(self):
-        for dx in (1, 3, 2):
-            x = lax.rem(self.x - dx + 4, 4)
-            arrived(self.full.at[self.rows(self.got, x), self.cols(self.y)], self.xsem.at[dx])
-        strip = self.strip(self.y)
-        for dy in (4, 3, 5, 2, 6, 1, 7):
-            remote(strip, strip, self.ssem.at[1], self.ysem.at[dy], at(dy, 0, 0, 0, 0)).start()
-
-    def finish_y_second(self):
-        for dy in (1, 7, 2, 6, 3, 5, 4):
-            arrived(self.strip(lax.rem(self.y - dy + 8, 8)), self.ysem.at[dy])
-        quarter = self.full.at[pl.ds(pl.multiple_of(self.got * 256, 256), 256)]
-        remote(quarter, quarter, self.ssem.at[3], self.dsem.at[1], at(0, 0, 0, 0, 1)).start()
-
-    def wait_sent_x_first(self):
-        left(self.full.at[pl.ds(0, 64), pl.ds(0, 128)], self.ssem.at[0])
-        left(self.full.at[pl.ds(0, 256), pl.ds(0, 896)], self.ssem.at[1])
-        left(self.full.at[pl.ds(0, 64), pl.ds(0, 384)], self.ssem.at[2])
+            arrived(self.full.at[self.rows(self.got, self.x_of(dx)), pl.ds(0, 256)], self.x1.at[dx])
+        for half in range(2):
+            self.along_y(self.strip(self.yq, half), 2, self.y2)
+
+    def finish_slow(self):
+        for dy in (1, 7, 2):
+            arrived(self.full.at[self.quarter(self.got), pl.ds(0, 256)], self.y2.at[dy])
+        self.hand_over(self.full.at[self.quarter(self.got)], 1)
+
+    def wait_sent_slow(self):
+        left(self.full.at[pl.ds(0, 64), pl.ds(0, 256)], self.ssem.at[0])
+        left(self.full.at[pl.ds(0, 64), pl.ds(0, 768)], self.ssem.at[1])
+        left(self.full.at[pl.ds(0, 256), pl.ds(0, 768)], self.ssem.at[2])
         left(self.full.at[pl.ds(0, 512)], self.ssem.at[3])
 
     def wait_all(self):
@@ -147,43 +178,66 @@
         arrived(quarter, self.dsem.at[0])
         arrived(quarter, self.dsem.at[1])
 
-    def wait_sent(self):
-        left(self.full.at[pl.ds(0, 64), pl.ds(0, 128)], self.ssem.at[0])
-        left(self.full.at[pl.ds(0, 64), pl.ds(0, 896)], self.ssem.at[1])
-        left(self.full.at[pl.ds(0, 192)], self.ssem.at[2])
-        left(self.full.at[pl.ds(0, 512)], self.ssem.at[3])
-
 
 def kernel(
-    ids_ref, remask_ref, mask_embed_ref, gain_in_ref, gain_out_ref, table_hbm, wqkv_hbm, wout_hbm, pos_hbm,
-    logp_ref, conf_ref, stats_ref,
-    table, wout, wqkv, pos, hidden, normed, kv_out, q_out, kv, q_in, qpad, high, total, summed, o_out, ctx,
+    ids_hbm, remask_hbm, mask_hbm, gain_in_hbm, gain_out_hbm, table_hbm, wqkv_hbm, wout_hbm, pos_hbm,
+    logp_hbm, conf_hbm, stats_hbm,
+    ids_ref, remask_ref, mask_embed_ref, gain_in_ref, gain_out_ref, logp_ref, conf_ref, stats_ref,
+    table_first, wout_first, table, wout, wqkv, pos, hidden, normed, kv_out, q_out, kv, q_in, qpad, high, total, summed, o_out, ctx,
     final, logits, weight, stat_out, stat_in,
-    local_sem, t_s, t_z, t_y, t_x, t_d, w_s, w_z, w_y, w_x, w_d, a_send, a_recv, q_recv, b_send, b_recv,
+    local_sem, small_sem, put_sem,
+    t_s, t_z, t_y1, t_x1, t_y2, t_x2, t_d, w_s, w_z, w_y1, w_x1, w_y2, w_x2, w_d,
+    a_send, a_recv, q_recv, b_send, b_recv,
     c_send, c_recv, f_send, f_recv, s_send, s_recv,
 ):
     y, zl, x, zh, core = coords()
     mp = zh * 2 + core
     frame = zl * 4 + x
-    tab = Spread(table_hbm, table, t_s, t_z, t_y, t_x, t_d)
-    out = Spread(wout_hbm, wout, w_s, w_z, w_y, w_x, w_d)
+    pair_z = (zl, zl + 1 - 2 * lax.rem(zl, 2), lax.rem(zl + 2, 4), 3 - zl)
+    tab = Spread(table_hbm, table, table_first, t_s, t_z, t_y1, t_x1, t_y2, t_x2, t_d)
+    out = Spread(wout_hbm, wout, wout_first, w_s, w_z, w_y1, w_x1, w_y2, w_x2, w_d)
     load_pos = pltpu.make_async_copy(pos_hbm.at[0], pos, local_sem.at[0])
     load_qkv = pltpu.make_async_copy(wqkv_hbm, wqkv, local_sem.at[1])
 
+    small = [
+        pltpu.make_async_copy(src, dst, small_sem.at[k])
+        for k, (src, dst) in enumerate(
+            (
+                (ids_hbm, ids_ref),
+                (remask_hbm, remask_ref),
+                (mask_hbm, mask_embed_ref),
+                (gain_in_hbm, gain_in_ref),
+                (gain_out_hbm, gain_out_ref),
+            )
+        )
+    ]
+    for half in range(2):
+        tab.fetch(half).start()
     barrier = pltpu.get_barrier_semaphore()
     peers = []
     for k in range(1, 16):
         place = lax.rem(zh * 8 + zl * 2 + core + k, 16)
         peers.append((y, lax.rem(place // 2, 4), x, place // 8, lax.rem(place, 2)))
-    peers += [at(k, 0, 0, 0, 0) for k in range(1, 8)]
+    peers += [at(k, 0, 0, 0, 0) for k in (1, 2, 6, 7)]
     peers += [at(0, dz, dx, 0, dc) for dx in range(1, 4) for dz in range(4) for dc in range(2)]
     for peer in peers:
         pl.semaphore_signal(barrier, inc=1, device_id=peer, device_id_type=MESH)
     tab.local().start()
+    for copy in small:
+        copy.start()
     load_pos.start()
+    out.local().start()
+    for half in range(2):
+        out.fetch(half).start()
     load_qkv.start()
-    out.local().start()
-
+    for half in range(2):
+        tab.fetch(half).wait()
+    pl.semaphore_wait(barrier, len(peers))
+    tab.start_z()
+    tab.local().wait()
+    tab.start_own_quarter()
+    for copy in small:
+        copy.wait()
     row = lax.broadcasted_iota(jnp.int32, (256, 256), 0)
     lane = lax.broadcasted_iota(jnp.int32, (256, 256), 1)
     masked = jnp.max(jnp.where(remask_ref[...] == row, 1.0, 0.0), axis=1, keepdims=True)
@@ -204,19 +258,17 @@
     for k in range(4):
         block = slice(k * 64, k * 64 + 64)
         hidden[block] = pos[block].astype(F32) + jnp.where(masked[block] > 0.5, mask_row, 0.0)
-    tab.local().wait()
-    out.local().wait()
-    pl.semaphore_wait(barrier, len(peers))
-    tab.start_z()
-    tab.start_own_quarter()
+    tab.begin()
+    for half in range(2):
+        out.fetch(half).wait()
     out.start_z()
-    tab.start_y()
     arrived(table.at[pl.ds(0, 256)], tab.dsem.at[0])
     hidden[...] += looked_up(zh)
-    tab.start_x()
-    out.start_x_first()
-    tab.finish_x()
-    out.start_y_second()
+    tab.forward()
+    out.begin_slow()
+    tab.finish()
+    out.forward_slow()
+    out.local().wait()
     out.start_own_quarter()
     load_qkv.wait()
     arrived(table.at[pl.ds(0, 256)], tab.dsem.at[1])
@@ -245,16 +297,22 @@
             remote(block, kv.at[s, slot], b_send.at[0], b_recv.at[s, slot], at(0, 0, dx, 0, 0)).start()
 
     pass_on(kv_out.at[zl], 0)
-    for dz in (1, 3, 2):
-        head = lax.rem(zl + dz, 4)
+    def send_keys(d):
         remote(
-            q_out.at[head], q_in.at[4 - dz], a_send.at[1], q_recv.at[4 - dz], at(0, dz, 0, 0, 0)
+            kv_out.at[pair_z[d]], kv.at[d, 0], a_send.at[0], a_recv.at[d], (y, pair_z[d], x, zh, core)
         ).start()
-    for dz in (3, 1, 2):
-        head = lax.rem(zl + dz, 4)
+
+    def send_query(d):
         remote(
-            kv_out.at[head], kv.at[4 - dz, 0], a_send.at[0], a_recv.at[4 - dz], at(0, dz, 0, 0, 0)
+            q_out.at[pair_z[d]], q_in.at[d], a_send.at[1], q_recv.at[d], (y, pair_z[d], x, zh, core)
         ).start()
+
+    send_keys(2)
+    send_keys(1)
+    send_query(1)
+    send_query(2)
+    send_keys(3)
+    send_query(3)
     kv[0, 0] = kv_out[zl]
 
     def unpack(k, packed):
@@ -266,17 +324,21 @@
     low64 = low[:64]
     head_here = mp * 4 + zl
 
+    def take(s):
+        arrived(kv.at[s, 0], a_recv.at[s])
+        pass_on(kv.at[s, 0], s)
+
+    held = set()
+
     def ready(s, b):
-        if s == 0:
-            if b == 0:
-                for slot in (1, 2, 3):
-                    arrived(kv.at[0, slot], b_recv.at[0, slot])
-            else:
-                arrived(q_in.at[b], q_recv.at[b])
-                unpack(b, q_in[b])
-        elif b == 0:
+        if b and (b, "q") not in held:
+            arrived(q_in.at[b], q_recv.at[b])
+            unpack(b, q_in[b])
+            held.add((b, "q"))
+        if s not in held:
             for slot in (1, 2, 3):
                 arrived(kv.at[s, slot], b_recv.at[s, slot])
+            held.add(s)
 
     def score(s, b):
         return lax.dot_general(
@@ -298,7 +360,7 @@
         w = jnp.exp2(scores * SCALE - now[:, :1] * SCALE)
         sums = total[b] * fade + jnp.sum(w, axis=1, keepdims=True)
         acc = summed[b] * fade + jnp.dot(w.astype(BF), rows, preferred_element_type=F32)
-        if s != 2:
+        if s != 3:
             high[b], total[b], summed[b] = now, sums, acc
             return
         rows = acc / sums
@@ -313,25 +375,28 @@
                 if b == 0 and dh == 0 and dc == 0:
                     continue
                 half = lax.rem(core + dc, 2)
+                there = (y, pair_z[b], x, lax.rem(zh + dh, 2), half)
                 remote(
-                    o_out.at[b, half], ctx.at[head_here], c_send.at[0], c_recv.at[0], at(0, b, 0, dh, dc)
+                    o_out.at[b, half], ctx.at[head_here], c_send.at[0], c_recv.at[0], there
                 ).start()
 
-    steps = [(s, b) for s in (0, 1, 3, 2) for b in (0, 1, 3, 2)]
+    steps = [(s, b) for s in (0, 2) for b in (0, 1, 2)] + [(0, 3), (2, 3)]
+    steps += [(s, b) for s in (1, 3) for b in (2, 3, 1, 0)]
+    take(2)
+    take(1)
     ready(0, 0)
     scores = score(0, 0)
     for i, (s, b) in enumerate(steps):
-        for arriving in {(0, 2): (1, 3), (1, 1): (2,)}.get((s, b), ()):
-            arrived(kv.at[arriving, 0], a_recv.at[arriving])
-            pass_on(kv.at[arriving, 0], arriving)
         if i + 1 < len(steps):
+            if steps[i + 1] == (2, 0):
+                take(3)
             ready(*steps[i + 1])
             following = score(*steps[i + 1])
         absorb(s, b, scores)
-        if s == 2:
+        if s == 3:
             send_context(b)
         scores = following
-    out.finish_y_second()
+    out.finish_slow()
     ctx[head_here] = o_out[0, core]
     out.wait_all()
     arrived(ctx.at[pl.ds(0, 15)], c_recv.at[0])
@@ -368,7 +433,7 @@
         for q in range(4):
             sums = sums + jnp.sum(jnp.exp(logits[q, block] - top), axis=1, keepdims=True)
         lse = top + jnp.log(sums)
-        logp_ref[0, block] = (logits[mp, block] - lse).astype(BF)
+        logp_ref[block] = (logits[mp, block] - lse).astype(BF)
         conf = jnp.exp(top - lse)
         high[0, block] = jnp.broadcast_to(conf, (128, 128))
         return conf
@@ -393,8 +458,15 @@
     arrived(final.at[other], f_recv.at[0])
     finish(other)
     conf_ref[...] = jnp.sum(jnp.where(row == lane, high[0][:, :1], 0.0), axis=0, keepdims=True)
+    put = [
+        pltpu.make_async_copy(logp_ref, logp_hbm.at[0], put_sem.at[0]),
+        pltpu.make_async_copy(conf_ref, conf_hbm, put_sem.at[1]),
+        pltpu.make_async_copy(stats_ref, stats_hbm, put_sem.at[2]),
+    ]
+    put[0].start()
+    put[1].start()
     tab.wait_sent()
-    out.wait_sent_x_first()
+    out.wait_sent_slow()
     left(kv_out.at[pl.ds(0, 3)], a_send.at[0])
     left(q_out.at[pl.ds(0, 3)], a_send.at[1])
     left(kv.at[pl.ds(0, 3)], b_send.at[0])
@@ -410,6 +482,9 @@
     all_conf = jnp.sum(jnp.where(lane1 == 0, sums, 0.0), axis=1, keepdims=True)
     all_count = jnp.sum(jnp.where(lane1 == 1, sums, 0.0), axis=1, keepdims=True)
     stats_ref[...] = jnp.where(lane1 == 0, all_conf / all_count, jnp.log(all_count / 4096.0))
+    put[2].start()
+    for copy in put:
+        copy.wait()
 
 
 def write_out(logp, conf, stats, logp_out, conf_out, stats_out):
@@ -422,7 +497,7 @@
     vmem = pl.BlockSpec(memory_space=pltpu.VMEM)
     hbm = pl.BlockSpec(memory_space=pl.ANY)
     dma = pltpu.SemaphoreType.DMA
-    spread_sems = [dma((5,)), dma, dma((8,)), dma((4,)), dma((2,))]
+    spread_sems = [dma((7,)), dma((2,)), dma((8,)), dma((4,)), dma((8,)), dma((4,)), dma((2,))]
     log_probs, confidence, stats = pl.pallas_call(
         kernel,
         out_shape=(
@@ -430,9 +505,19 @@
             jax.ShapeDtypeStruct((1, 256), F32),
             jax.ShapeDtypeStruct((1, 128), F32),
         ),
-        in_specs=[vmem] * 5 + [hbm] * 4,
-        out_specs=(vmem, vmem, vmem),
+        in_specs=[hbm] * 9,
+        out_specs=(hbm, hbm, hbm),
         scratch_shapes=[
+            pltpu.VMEM((1, 256), jnp.int32),
+            pltpu.VMEM((1, 256), jnp.int32),
+            pltpu.VMEM((1024,), BF),
+            pltpu.VMEM((1, 1024), F32),
+            pltpu.VMEM((1, 1024), F32),
+            pltpu.VMEM((256, 256), BF),
+            pltpu.VMEM((1, 256), F32),
+            pltpu.VMEM((1, 128), F32),
+            pltpu.VMEM((2, 64, 128), BF),
+            pltpu.VMEM((2, 64, 128), BF),
             pltpu.VMEM((1024, 1024), BF),
             pltpu.VMEM((1024, 1024), BF),
             pltpu.VMEM((3, 1024, 256), BF),
@@ -455,6 +540,8 @@
             pltpu.VMEM((8, 128), F32),
             pltpu.VMEM((32, 8, 128), F32),
             dma((2,)),
+            dma((5,)),
+            dma((3,)),
             *spread_sems,
             *spread_sems,
             dma((2,)),

time: 72 us -> 67.3 us (0.935)
  Pallas kernels: 71.1 us -> 66.5 us
    pallas_call x1, Pallas kernels: 69.5 us -> 64.9 us  [body(): pl.pallas_call(kernel, out_shape=(jax.ShapeDtypeStruct((1, 256, 256), BF)...]
where the time goes in v3:
time: 67.3 us; the launch traced here: 67.1 us
  Pallas kernels  66.5 us (99%)
    pallas_call x1, Pallas kernels, body(): pl.pallas_call(kernel, out_shape=(jax.ShapeDtypeStruct((1, 256, 256), BF)...  64.9 us
    pallas_call x1, Pallas kernels, body(): pl.pallas_call(write_out, out_shape=(jax.ShapeDtypeStruct((1, 256, 256),...  1.58 us

profile of v3, /device:TPU:1, one launch (start us, length us, event | category | flops | bytes accessed | tf_op | source)
XLA Modules:
  0.0 67.1 jit_solution(9324284800378779270)
XLA Ops:
  0.6 64.9 %predict.1 = (bf16[1,256,256]{2,1,0:T(8,128)(2,1)}, f32[1,256]{1,0:T(1,128)}, f32[1,128]{1,0:T(1,128)}) custom-call(s32[1,256]{1,0:T(1,128)} %ids_hbm.1, s32[1,256]{1,0:T(1,128)} %remask_hbm.1, bf16[1024]{0:T(1024)(128)(2,1)} %mask_hbm.1, f32[1,1024]{1,0:T(1,128)} %bitcast.3, f32[1,1024]{1,0:T(1,128)} %bitcast.4, bf16[256,1024]{1,0:T(8,128)(2,1)} %table_hbm.1, ...), custom_call_target="tpu_custom_call" | custom-call | tf_op jit(solution)/shard_map/predict/pallas_call | solution.py:501
  65.6 1.6 %write_out.1 = (bf16[1,256,256]{2,1,0:T(8,128)(2,1)}, f32[1,256]{1,0:T(1,128)}, f32[1,2]{1,0:T(1,128)}) custom-call(bf16[1,256,256]{2,1,0:T(8,128)(2,1)} %get-tuple-element.9.logp, f32[1,256]{1,0:T(1,128)} %get-tuple-element.10.conf, f32[1,128]{1,0:T(1,128)} %get-tuple-element.11.stats), custom_call_target="tpu_custom_call" | custom-call | tf_op jit(solution)/shard_map/write_out/pallas_call | solution.py:574

commit v4 on v3

--- a/solution.py
+++ b/solution.py
@@ -183,7 +183,7 @@
     ids_hbm, remask_hbm, mask_hbm, gain_in_hbm, gain_out_hbm, table_hbm, wqkv_hbm, wout_hbm, pos_hbm,
     logp_hbm, conf_hbm, stats_hbm,
     ids_ref, remask_ref, mask_embed_ref, gain_in_ref, gain_out_ref, logp_ref, conf_ref, stats_ref,
-    table_first, wout_first, table, wout, wqkv, pos, hidden, normed, kv_out, q_out, kv, q_in, qpad, high, total, summed, o_out, ctx,
+    table_first, wout_first, flipped, table, wout, wqkv, pos, hidden, normed, kv_out, q_out, kv, q_in, qpad, high, total, summed, o_out, ctx,
     final, logits, weight, stat_out, stat_in,
     local_sem, small_sem, put_sem,
     t_s, t_z, t_y1, t_x1, t_y2, t_x2, t_d, w_s, w_z, w_y1, w_x1, w_y2, w_x2, w_d,
@@ -246,12 +246,12 @@
     )
     weight[...] = jnp.broadcast_to(masked, (256, 128))
     ids_col = jnp.where(masked > 0.5, -1.0, ids_col)
-    entry = lax.broadcasted_iota(jnp.int32, (256, 512), 1)
     mask_row = mask_embed_ref[...].astype(F32).reshape(1, 1024)
 
-    def looked_up(half):
-        onehot = jnp.where((entry + half * 512).astype(F32) == ids_col, 1.0, 0.0).astype(BF)
-        rows = table[pl.ds(pl.multiple_of(half * 512, 512), 512)]
+    def looked_up(first, count):
+        entry = lax.broadcasted_iota(jnp.int32, (256, count), 1) + first
+        onehot = jnp.where(entry.astype(F32) == ids_col, 1.0, 0.0).astype(BF)
+        rows = table[pl.ds(pl.multiple_of(first, count), count)]
         return jnp.dot(onehot, rows, preferred_element_type=F32)
 
     load_pos.wait()
@@ -263,7 +263,7 @@
         out.fetch(half).wait()
     out.start_z()
     arrived(table.at[pl.ds(0, 256)], tab.dsem.at[0])
-    hidden[...] += looked_up(zh)
+    hidden[...] += looked_up(zh * 512, 512)
     tab.forward()
     out.begin_slow()
     tab.finish()
@@ -271,8 +271,9 @@
     out.local().wait()
     out.start_own_quarter()
     load_qkv.wait()
+    hidden[...] += looked_up((2 - 2 * zh + core) * 256, 256)
     arrived(table.at[pl.ds(0, 256)], tab.dsem.at[1])
-    hidden[...] += looked_up(1 - zh)
+    hidden[...] += looked_up((3 - 2 * zh - core) * 256, 256)
     gain_in = gain_in_ref[...]
     for k in range(4):
         block = slice(k * 64, k * 64 + 64)
@@ -291,15 +292,20 @@
         qa, qb = query[:128, g * 128 : g * 128 + 128], query[128:, g * 128 : g * 128 + 128]
         q_out[2 * g] = jnp.where(low_half, qa, pltpu.roll(qb, 64, 1)).astype(BF)
         q_out[2 * g + 1] = jnp.where(low_half, pltpu.roll(qa, 64, 1), qb).astype(BF)
+    def spot(s, slot):
+        return (0, 2, 1, 3)[s] * 4 + slot
+
+    chunk = {0: slice(0, 4), 2: slice(4, 8), 1: slice(8, 13), 3: slice(13, 16)}
+
     def pass_on(block, s):
         for dx in (1, 3, 2):
             slot = (0, 1, 3, 2)[dx]
-            remote(block, kv.at[s, slot], b_send.at[0], b_recv.at[s, slot], at(0, 0, dx, 0, 0)).start()
+            remote(block, kv.at[spot(s, slot)], b_send.at[0], b_recv.at[s, slot], at(0, 0, dx, 0, 0)).start()
 
     pass_on(kv_out.at[zl], 0)
     def send_keys(d):
         remote(
-            kv_out.at[pair_z[d]], kv.at[d, 0], a_send.at[0], a_recv.at[d], (y, pair_z[d], x, zh, core)
+            kv_out.at[pair_z[d]], kv.at[spot(d, 0)], a_send.at[0], a_recv.at[d], (y, pair_z[d], x, zh, core)
         ).start()
 
     def send_query(d):
@@ -313,7 +319,7 @@
     send_query(2)
     send_keys(3)
     send_query(3)
-    kv[0, 0] = kv_out[zl]
+    kv[spot(0, 0)] = kv_out[zl]
 
     def unpack(k, packed):
         packed = packed.astype(F32)
@@ -325,8 +331,8 @@
     head_here = mp * 4 + zl
 
     def take(s):
-        arrived(kv.at[s, 0], a_recv.at[s])
-        pass_on(kv.at[s, 0], s)
+        arrived(kv.at[spot(s, 0)], a_recv.at[s])
+        pass_on(kv.at[spot(s, 0)], s)
 
     held = set()
 
@@ -337,16 +343,16 @@
             held.add((b, "q"))
         if s not in held:
             for slot in (1, 2, 3):
-                arrived(kv.at[s, slot], b_recv.at[s, slot])
+                arrived(kv.at[spot(s, slot)], b_recv.at[s, slot])
             held.add(s)
 
     def score(s, b):
         return lax.dot_general(
-            qpad[b], kv[s].reshape(1024, 128), (((1,), (1,)), ((), ())), preferred_element_type=F32
+            qpad[b], kv[chunk[s]].reshape(-1, 128), (((1,), (1,)), ((), ())), preferred_element_type=F32
         )
 
     def absorb(s, b, scores):
-        rows = kv[s].reshape(1024, 128)
+        rows = kv[chunk[s]].reshape(-1, 128)
         top = jnp.max(scores, axis=1, keepdims=True)
         if s == 0:
             w = jnp.exp2(scores * SCALE - top * SCALE)
@@ -396,9 +402,12 @@
         if s == 3:
             send_context(b)
         scores = following
+    ctx[head_here] = o_out[0, core]
     out.finish_slow()
-    ctx[head_here] = o_out[0, core]
+    for q in range(4):
+        flipped[:, q * 256 : q * 256 + 256] = table[q * 256 : q * 256 + 256].T
     out.wait_all()
+
     arrived(ctx.at[pl.ds(0, 15)], c_recv.at[0])
     pieces = []
     for g in range(8):
@@ -423,9 +432,7 @@
         rows = final[block]
         tops = []
         for q in range(4):
-            part = lax.dot_general(
-                rows, table[q * 256 : q * 256 + 256], (((1,), (1,)), ((), ())), preferred_element_type=F32
-            )
+            part = jnp.dot(rows, flipped[:, q * 256 : q * 256 + 256], preferred_element_type=F32)
             logits[q, block] = part
             tops.append(jnp.max(part, axis=1, keepdims=True))
         top = jnp.maximum(jnp.maximum(tops[0], tops[1]), jnp.maximum(tops[2], tops[3]))
@@ -433,17 +440,19 @@
         for q in range(4):
             sums = sums + jnp.sum(jnp.exp(logits[q, block] - top), axis=1, keepdims=True)
         lse = top + jnp.log(sums)
-        logp_ref[block] = (logits[mp, block] - lse).astype(BF)
         conf = jnp.exp(top - lse)
         high[0, block] = jnp.broadcast_to(conf, (128, 128))
-        return conf
-
-    conf = finish(mine)
+        return conf, lse
+
+    def put_rows(block, lse):
+        logp_ref[block] = (logits[mp, block] - lse).astype(BF)
+
+    conf, lse = finish(mine)
     w = weight[mine][:, :1]
-    lane8 = lax.broadcasted_iota(jnp.int32, (8, 128), 1)
+    lane1 = lax.broadcasted_iota(jnp.int32, (1, 128), 1)
     conf_sum = jnp.sum(conf * w, axis=0, keepdims=True)
     count = jnp.sum(w, axis=0, keepdims=True)
-    tile = jnp.where(lane8 == 0, conf_sum, jnp.where(lane8 == 1, count, 0.0))
+    tile = jnp.where(lane1 == 0, conf_sum, jnp.where(lane1 == 1, count, 0.0))
     place = frame * 2 + core
     stat_out[...] = tile
     stat_in[place] = tile
@@ -454,9 +463,11 @@
                     remote(
                         stat_out, stat_in.at[place], s_send.at[0], s_recv.at[0], at(0, dz, dx, 0, dc)
                     ).start()
+    put_rows(mine, lse)
     other = pl.ds(pl.multiple_of((1 - core) * 128, 128), 128)
     arrived(final.at[other], f_recv.at[0])
-    finish(other)
+    conf, lse = finish(other)
+    put_rows(other, lse)
     conf_ref[...] = jnp.sum(jnp.where(row == lane, high[0][:, :1], 0.0), axis=0, keepdims=True)
     put = [
         pltpu.make_async_copy(logp_ref, logp_hbm.at[0], put_sem.at[0]),
@@ -469,7 +480,7 @@
     out.wait_sent_slow()
     left(kv_out.at[pl.ds(0, 3)], a_send.at[0])
     left(q_out.at[pl.ds(0, 3)], a_send.at[1])
-    left(kv.at[pl.ds(0, 3)], b_send.at[0])
+    left(kv.at[pl.ds(0, 12)], b_send.at[0])
     left(ctx.at[pl.ds(0, 15)], c_send.at[0])
     send_final.wait_send()
     arrived(stat_in.at[pl.ds(0, 31)], s_recv.at[0])
@@ -477,8 +488,6 @@
     sums = stat_in[0]
     for k in range(1, 32):
         sums = sums + stat_in[k]
-    sums = sums[:1]
-    lane1 = lane8[:1]
     all_conf = jnp.sum(jnp.where(lane1 == 0, sums, 0.0), axis=1, keepdims=True)
     all_count = jnp.sum(jnp.where(lane1 == 1, sums, 0.0), axis=1, keepdims=True)
     stats_ref[...] = jnp.where(lane1 == 0, all_conf / all_count, jnp.log(all_count / 4096.0))
@@ -520,13 +529,14 @@
             pltpu.VMEM((2, 64, 128), BF),
             pltpu.VMEM((1024, 1024), BF),
             pltpu.VMEM((1024, 1024), BF),
+            pltpu.VMEM((1024, 1024), BF),
             pltpu.VMEM((3, 1024, 256), BF),
             pltpu.VMEM((256, 1024), BF),
             pltpu.VMEM((256, 1024), F32),
             pltpu.VMEM((256, 1024), BF),
             pltpu.VMEM((4, 256, 128), BF),
             pltpu.VMEM((4, 128, 128), BF),
-            pltpu.VMEM((4, 4, 256, 128), BF),
+            pltpu.VMEM((16, 256, 128), BF),
             pltpu.VMEM((4, 128, 128), BF),
             pltpu.VMEM((4, 256, 128), BF),
             pltpu.VMEM((4, 256, 128), F32),
@@ -537,8 +547,8 @@
             pltpu.VMEM((256, 1024), BF),
             pltpu.VMEM((4, 256, 256), F32),
             pltpu.VMEM((256, 128), F32),
-            pltpu.VMEM((8, 128), F32),
-            pltpu.VMEM((32, 8, 128), F32),
+            pltpu.VMEM((1, 128), F32),
+            pltpu.VMEM((32, 1, 128), F32),
             dma((2,)),
             dma((5,)),
             dma((3,)),

time: 67.3 us -> 66.8 us (level)
  no operation moved by 1% of the time
where the time goes in v4:
time: 66.8 us; the launch traced here: 66.7 us
  Pallas kernels  66 us (99%)
    pallas_call x1, Pallas kernels, body(): pl.pallas_call(kernel, out_shape=(jax.ShapeDtypeStruct((1, 256, 256), BF)...  64.4 us
    pallas_call x1, Pallas kernels, body(): pl.pallas_call(write_out, out_shape=(jax.ShapeDtypeStruct((1, 256, 256),...  1.58 us

profile of v4, /device:TPU:1, one launch (start us, length us, event | category | flops | bytes accessed | tf_op | source)
XLA Modules:
  0.0 66.7 jit_solution(1317906543463628469)
XLA Ops:
  0.6 64.4 %predict.1 = (bf16[1,256,256]{2,1,0:T(8,128)(2,1)}, f32[1,256]{1,0:T(1,128)}, f32[1,128]{1,0:T(1,128)}) custom-call(s32[1,256]{1,0:T(1,128)} %ids_hbm.1, s32[1,256]{1,0:T(1,128)} %remask_hbm.1, bf16[1024]{0:T(1024)(128)(2,1)} %mask_hbm.1, f32[1,1024]{1,0:T(1,128)} %bitcast.3, f32[1,1024]{1,0:T(1,128)} %bitcast.4, bf16[256,1024]{1,0:T(8,128)(2,1)} %table_hbm.1, ...), custom_call_target="tpu_custom_call" | custom-call | tf_op jit(solution)/shard_map/predict/pallas_call | solution.py:510
  65.1 1.6 %write_out.1 = (bf16[1,256,256]{2,1,0:T(8,128)(2,1)}, f32[1,256]{1,0:T(1,128)}, f32[1,2]{1,0:T(1,128)}) custom-call(bf16[1,256,256]{2,1,0:T(8,128)(2,1)} %get-tuple-element.9.logp, f32[1,256]{1,0:T(1,128)} %get-tuple-element.10.conf, f32[1,128]{1,0:T(1,128)} %get-tuple-element.11.stats), custom_call_target="tpu_custom_call" | custom-call | tf_op jit(solution)/shard_map/write_out/pallas_call | solution.py:584

commit v5 on v4

--- a/solution.py
+++ b/solution.py
@@ -181,11 +181,11 @@
 
 def kernel(
     ids_hbm, remask_hbm, mask_hbm, gain_in_hbm, gain_out_hbm, table_hbm, wqkv_hbm, wout_hbm, pos_hbm,
-    logp_hbm, conf_hbm, stats_hbm,
-    ids_ref, remask_ref, mask_embed_ref, gain_in_ref, gain_out_ref, logp_ref, conf_ref, stats_ref,
+    logp_ref, conf_ref, stats_ref,
+    ids_ref, remask_ref, mask_embed_ref, gain_in_ref, gain_out_ref,
     table_first, wout_first, flipped, table, wout, wqkv, pos, hidden, normed, kv_out, q_out, kv, q_in, qpad, high, total, summed, o_out, ctx,
     final, logits, weight, stat_out, stat_in,
-    local_sem, small_sem, put_sem,
+    local_sem, small_sem,
     t_s, t_z, t_y1, t_x1, t_y2, t_x2, t_d, w_s, w_z, w_y1, w_x1, w_y2, w_x2, w_d,
     a_send, a_recv, q_recv, b_send, b_recv,
     c_send, c_recv, f_send, f_recv, s_send, s_recv,
@@ -469,13 +469,6 @@
     conf, lse = finish(other)
     put_rows(other, lse)
     conf_ref[...] = jnp.sum(jnp.where(row == lane, high[0][:, :1], 0.0), axis=0, keepdims=True)
-    put = [
-        pltpu.make_async_copy(logp_ref, logp_hbm.at[0], put_sem.at[0]),
-        pltpu.make_async_copy(conf_ref, conf_hbm, put_sem.at[1]),
-        pltpu.make_async_copy(stats_ref, stats_hbm, put_sem.at[2]),
-    ]
-    put[0].start()
-    put[1].start()
     tab.wait_sent()
     out.wait_sent_slow()
     left(kv_out.at[pl.ds(0, 3)], a_send.at[0])
@@ -490,16 +483,19 @@
         sums = sums + stat_in[k]
     all_conf = jnp.sum(jnp.where(lane1 == 0, sums, 0.0), axis=1, keepdims=True)
     all_count = jnp.sum(jnp.where(lane1 == 1, sums, 0.0), axis=1, keepdims=True)
-    stats_ref[...] = jnp.where(lane1 == 0, all_conf / all_count, jnp.log(all_count / 4096.0))
-    put[2].start()
-    for copy in put:
+    both = jnp.where(lane1 == 0, all_conf / all_count, jnp.log(all_count / 4096.0))
+    stats_ref[...] = both[:, :2]
+
+
+def write_out(logp, conf, stats, logp_out, conf_out, stats_out, sem):
+    copies = [
+        pltpu.make_async_copy(src, dst, sem.at[k])
+        for k, (src, dst) in enumerate(((logp, logp_out.at[0]), (conf, conf_out), (stats, stats_out)))
+    ]
+    for copy in copies:
+        copy.start()
+    for copy in copies:
         copy.wait()
-
-
-def write_out(logp, conf, stats, logp_out, conf_out, stats_out):
-    logp_out[...] = logp[...]
-    conf_out[...] = conf[...]
-    stats_out[...] = stats[:, :2]
 
 
 def body(token_ids, remask, position_embed, mask_embed, table, gain_in, gain_out, w_qkv, w_out):
@@ -510,21 +506,18 @@
     log_probs, confidence, stats = pl.pallas_call(
         kernel,
         out_shape=(
-            jax.ShapeDtypeStruct((1, 256, 256), BF),
-            jax.ShapeDtypeStruct((1, 256), F32),
-            jax.ShapeDtypeStruct((1, 128), F32),
+            pltpu.VMEM((256, 256), BF),
+            pltpu.VMEM((1, 256), F32),
+            pltpu.VMEM((1, 2), F32),
         ),
         in_specs=[hbm] * 9,
-        out_specs=(hbm, hbm, hbm),
+        out_specs=(vmem, vmem, vmem),
         scratch_shapes=[
             pltpu.VMEM((1, 256), jnp.int32),
             pltpu.VMEM((1, 256), jnp.int32),
             pltpu.VMEM((1024,), BF),
             pltpu.VMEM((1, 1024), F32),
             pltpu.VMEM((1, 1024), F32),
-            pltpu.VMEM((256, 256), BF),
-            pltpu.VMEM((1, 256), F32),
-            pltpu.VMEM((1, 128), F32),
             pltpu.VMEM((2, 64, 128), BF),
             pltpu.VMEM((2, 64, 128), BF),
             pltpu.VMEM((1024, 1024), BF),
@@ -551,7 +544,6 @@
             pltpu.VMEM((32, 1, 128), F32),
             dma((2,)),
             dma((5,)),
-            dma((3,)),
             *spread_sems,
             *spread_sems,
             dma((2,)),
@@ -589,7 +581,9 @@
             jax.ShapeDtypeStruct((1, 2), F32),
         ),
         in_specs=[vmem] * 3,
-        out_specs=(vmem, vmem, vmem),
+        out_specs=(hbm, hbm, hbm),
+        scratch_shapes=[dma((3,))],
+        compiler_params=pltpu.CompilerParams(vmem_limit_bytes=1024 * 1024),
         name="write_out",
     )(log_probs, confidence, stats)
     return log_probs, confidence, stats.reshape(2)

time: 66.8 us -> 65.3 us (0.978)
  Pallas kernels: 66 us -> 64.5 us
    pallas_call x1, Pallas kernels: 1.58 us -> 0.69 us  [body(): pl.pallas_call(write_out, out_shape=(jax.ShapeDtypeStruct((1, 256, 256),...]
where the time goes in v5:
time: 65.3 us; the launch traced here: 65.2 us
  Pallas kernels  64.5 us (99%)
    pallas_call x1, Pallas kernels, body(): pl.pallas_call(kernel, out_shape=(pltpu.VMEM((256, 256), BF), pltpu.VMEM(...  63.8 us

profile of v5, /device:TPU:1, one launch (start us, length us, event | category | flops | bytes accessed | tf_op | source)
XLA Modules:
  0.0 65.2 jit_solution(2997219644257794292)
XLA Ops:
  0.6 63.8 %predict.1 = (bf16[256,256]{1,0:T(8,128)(2,1)S(1)}, f32[1,256]{1,0:T(1,128)S(1)}, f32[1,2]{1,0:T(1,128)S(1)}) custom-call(s32[1,256]{1,0:T(1,128)} %ids_hbm.1, s32[1,256]{1,0:T(1,128)} %remask_hbm.1, bf16[1024]{0:T(1024)(128)(2,1)} %mask_hbm.1, f32[1,1024]{1,0:T(1,128)} %bitcast.3, f32[1,1024]{1,0:T(1,128)} %bitcast.4, bf16[256,1024]{1,0:T(8,128)(2,1)} %table_hbm.1, ...), custom_call_target="tpu_custom_call" | custom-call | tf_op jit(solution)/shard_map/predict/pallas_call | solution.py:506
  64.5 0.7 %write_out.1 = (bf16[1,256,256]{2,1,0:T(8,128)(2,1)}, f32[1,256]{1,0:T(1,128)}, f32[1,2]{1,0:T(1,128)}) custom-call(bf16[256,256]{1,0:T(8,128)(2,1)S(1)} %get-tuple-element.9.logp, f32[1,256]{1,0:T(1,128)S(1)} %get-tuple-element.10.conf, f32[1,2]{1,0:T(1,128)S(1)} %get-tuple-element.11.stats), custom_call_target="tpu_custom_call" | custom-call | tf_op jit(solution)/shard_map/write_out/pallas_call | solution.py:576

commit v6 on v5

--- a/solution.py
+++ b/solution.py
@@ -287,34 +287,34 @@
         kv_out[2 * g] = jnp.where(low, kg, pltpu.roll(vg, 64, 1)).astype(BF)
         kv_out[2 * g + 1] = jnp.where(low, pltpu.roll(kg, 64, 1), vg).astype(BF)
     query = jnp.dot(n_all, wqkv[0], preferred_element_type=F32)
+    def spot(s, slot):
+        return (0, 2, 1, 3)[s] * 4 + slot
+
+    chunk = {0: slice(0, 4), 2: slice(4, 8), 1: slice(8, 13), 3: slice(13, 16)}
+
+    def pass_on(block, s):
+        for dx in (2, 1, 3):
+            slot = (0, 1, 3, 2)[dx]
+            remote(block, kv.at[spot(s, slot)], b_send.at[0], b_recv.at[s, slot], at(0, 0, dx, 0, 0)).start()
+
+    pass_on(kv_out.at[zl], 0)
+    def send_keys(d):
+        remote(
+            kv_out.at[pair_z[d]], kv.at[spot(d, 0)], a_send.at[0], a_recv.at[d], (y, pair_z[d], x, zh, core)
+        ).start()
+
+    def send_query(d):
+        remote(
+            q_out.at[pair_z[d]], q_in.at[d], a_send.at[1], q_recv.at[d], (y, pair_z[d], x, zh, core)
+        ).start()
+
+    send_keys(2)
+    send_keys(1)
     low_half = low[:128]
     for g in range(2):
         qa, qb = query[:128, g * 128 : g * 128 + 128], query[128:, g * 128 : g * 128 + 128]
         q_out[2 * g] = jnp.where(low_half, qa, pltpu.roll(qb, 64, 1)).astype(BF)
         q_out[2 * g + 1] = jnp.where(low_half, pltpu.roll(qa, 64, 1), qb).astype(BF)
-    def spot(s, slot):
-        return (0, 2, 1, 3)[s] * 4 + slot
-
-    chunk = {0: slice(0, 4), 2: slice(4, 8), 1: slice(8, 13), 3: slice(13, 16)}
-
-    def pass_on(block, s):
-        for dx in (1, 3, 2):
-            slot = (0, 1, 3, 2)[dx]
-            remote(block, kv.at[spot(s, slot)], b_send.at[0], b_recv.at[s, slot], at(0, 0, dx, 0, 0)).start()
-
-    pass_on(kv_out.at[zl], 0)
-    def send_keys(d):
-        remote(
-            kv_out.at[pair_z[d]], kv.at[spot(d, 0)], a_send.at[0], a_recv.at[d], (y, pair_z[d], x, zh, core)
-        ).start()
-
-    def send_query(d):
-        remote(
-            q_out.at[pair_z[d]], q_in.at[d], a_send.at[1], q_recv.at[d], (y, pair_z[d], x, zh, core)
-        ).start()
-
-    send_keys(2)
-    send_keys(1)
     send_query(1)
     send_query(2)
     send_keys(3)

time: 65.3 us -> 63.2 us (0.968)
  Pallas kernels: 64.5 us -> 62.4 us
    pallas_call x1, Pallas kernels: 63.8 us -> 61.7 us  [body(): pl.pallas_call(kernel, out_shape=(pltpu.VMEM((256, 256), BF), pltpu.VMEM(...]
where the time goes in v6:
time: 63.2 us; the launch traced here: 63 us
  Pallas kernels  62.4 us (99%)
  between operations  0.64 us (1%)
    pallas_call x1, Pallas kernels, body(): pl.pallas_call(kernel, out_shape=(pltpu.VMEM((256, 256), BF), pltpu.VMEM(...  61.7 us

profile of v6, /device:TPU:1, one launch (start us, length us, event | category | flops | bytes accessed | tf_op | source)
XLA Modules:
  0.0 63.0 jit_solution(8384647408895612170)
XLA Ops:
  0.6 61.7 %predict.1 = (bf16[256,256]{1,0:T(8,128)(2,1)S(1)}, f32[1,256]{1,0:T(1,128)S(1)}, f32[1,2]{1,0:T(1,128)S(1)}) custom-call(s32[1,256]{1,0:T(1,128)} %ids_hbm.1, s32[1,256]{1,0:T(1,128)} %remask_hbm.1, bf16[1024]{0:T(1024)(128)(2,1)} %mask_hbm.1, f32[1,1024]{1,0:T(1,128)} %bitcast.3, f32[1,1024]{1,0:T(1,128)} %bitcast.4, bf16[256,1024]{1,0:T(8,128)(2,1)} %table_hbm.1, ...), custom_call_target="tpu_custom_call" | custom-call | tf_op jit(solution)/shard_map/predict/pallas_call | solution.py:506
  62.3 0.7 %write_out.1 = (bf16[1,256,256]{2,1,0:T(8,128)(2,1)}, f32[1,256]{1,0:T(1,128)}, f32[1,2]{1,0:T(1,128)}) custom-call(bf16[256,256]{1,0:T(8,128)(2,1)S(1)} %get-tuple-element.9.logp, f32[1,256]{1,0:T(1,128)S(1)} %get-tuple-element.10.conf, f32[1,2]{1,0:T(1,128)S(1)} %get-tuple-element.11.stats), custom_call_target="tpu_custom_call" | custom-call | tf_op jit(solution)/shard_map/write_out/pallas_call | solution.py:576

commit v7 on v6

--- a/solution.py
+++ b/solution.py
@@ -286,7 +286,6 @@
         kg, vg = keys[:, g * 128 : g * 128 + 128], values[:, g * 128 : g * 128 + 128]
         kv_out[2 * g] = jnp.where(low, kg, pltpu.roll(vg, 64, 1)).astype(BF)
         kv_out[2 * g + 1] = jnp.where(low, pltpu.roll(kg, 64, 1), vg).astype(BF)
-    query = jnp.dot(n_all, wqkv[0], preferred_element_type=F32)
     def spot(s, slot):
         return (0, 2, 1, 3)[s] * 4 + slot
 
@@ -310,6 +309,7 @@
 
     send_keys(2)
     send_keys(1)
+    query = jnp.dot(n_all, wqkv[0], preferred_element_type=F32)
     low_half = low[:128]
     for g in range(2):
         qa, qb = query[:128, g * 128 : g * 128 + 128], query[128:, g * 128 : g * 128 + 128]

time: 63.2 us -> 63.1 us (level)
  no operation moved by 1% of the time
where the time goes in v7:
time: 63.1 us; the launch traced here: 62.9 us
  Pallas kernels  62.3 us (99%)
  between operations  0.64 us (1%)
    pallas_call x1, Pallas kernels, body(): pl.pallas_call(kernel, out_shape=(pltpu.VMEM((256, 256), BF), pltpu.VMEM(...  61.6 us

profile of v7, /device:TPU:1, one launch (start us, length us, event | category | flops | bytes accessed | tf_op | source)
XLA Modules:
  0.0 62.9 jit_solution(3597199791531992639)
XLA Ops:
  0.6 61.6 %predict.1 = (bf16[256,256]{1,0:T(8,128)(2,1)S(1)}, f32[1,256]{1,0:T(1,128)S(1)}, f32[1,2]{1,0:T(1,128)S(1)}) custom-call(s32[1,256]{1,0:T(1,128)} %ids_hbm.1, s32[1,256]{1,0:T(1,128)} %remask_hbm.1, bf16[1024]{0:T(1024)(128)(2,1)} %mask_hbm.1, f32[1,1024]{1,0:T(1,128)} %bitcast.3, f32[1,1024]{1,0:T(1,128)} %bitcast.4, bf16[256,1024]{1,0:T(8,128)(2,1)} %table_hbm.1, ...), custom_call_target="tpu_custom_call" | custom-call | tf_op jit(solution)/shard_map/predict/pallas_call | solution.py:506
  62.2 0.7 %write_out.1 = (bf16[1,256,256]{2,1,0:T(8,128)(2,1)}, f32[1,256]{1,0:T(1,128)}, f32[1,2]{1,0:T(1,128)}) custom-call(bf16[256,256]{1,0:T(8,128)(2,1)S(1)} %get-tuple-element.9.logp, f32[1,256]{1,0:T(1,128)S(1)} %get-tuple-element.10.conf, f32[1,2]{1,0:T(1,128)S(1)} %get-tuple-element.11.stats), custom_call_target="tpu_custom_call" | custom-call | tf_op jit(solution)/shard_map/write_out/pallas_call | solution.py:576
